TPU v7x, 256 devices: a whole 4x4x8 slice. The times are simulated.
256 devices in a mesh: gx: 8 (over y, core), gy: 8 (over z), gz: 4 (over x).
Axes of the slice: x: 4, y: 4, z: 8, core: 2. Of those that a mesh axis runs over, the one named last changes fastest.
Arguments:
- density: float32 [256, 128, 512], P('gx', 'gy', 'gz'), may hold values from -8 to 8
Outputs:
- potential: float32 [256, 128, 512], P('gx', 'gy', 'gz')
All inputs are finite; a program needn't handle non-finite values.
Results may differ from a plain program's by a relative error of at most 0.00002.
Values sent between devices are 32-bit elements; how exact they have to be, the bound alone decides.
A program may use at most 128 MiB of HBM per device.

v0:
```python
import jax
import jax.numpy as jnp
from jax import lax
from jax.sharding import Mesh
from jax.sharding import PartitionSpec as P

LEVELS = 7
CSWEEPS = 4
GX_GY_GZ = ("gx_0", "gx_1", "gy", "gz")
GX = ("gx_0", "gx_1")


rsd_beta = 0.5
centre = 4.0 + 2.0 * (1.0 + rsd_beta)


def with_halo(value, sides, width):
    edges = {}
    for axis, dim in sides:
        count, length = (lax.axis_size(axis), value.shape[dim])
        up = [(i, (i + 1) % count) for i in range(count - 1)]
        last = lax.slice_in_dim(value, length - width, length, axis=dim)
        leading = lax.slice_in_dim(value, 0, width, axis=dim)
        edges[dim] = (
            lax.ppermute(last, axis, up),
            lax.ppermute(leading, axis, [(b, a) for a, b in up]),
        )
    done = []
    for _, dim in sides:
        low, high = edges[dim]
        around = [(width, width) if d in done else (0, 0) for d in range(value.ndim)]
        value = jnp.concatenate([jnp.pad(low, around), value, jnp.pad(high, around)], axis=dim)
        done.append(dim)
    return value


def extended_2(value, sides, width):
    for axis, dim in sides:
        count, length = (lax.axis_size(axis), value.shape[dim])
        up = [(i, (i + 1) % count) for i in range(count - 1)]
        down = [(j, i) for i, j in up]
        last = lax.slice_in_dim(value, length - width, length, axis=dim)
        leading = lax.slice_in_dim(value, 0, width, axis=dim)
        before = lax.ppermute(last, axis, up)
        after = lax.ppermute(leading, axis, down)
        value = jnp.concatenate([before, value, after], axis=dim)
    return value


def joined_along(pieces, dim):
    dims = list(pieces.shape[1:])
    dims[dim] *= pieces.shape[0]
    return jnp.moveaxis(pieces, 0, dim).reshape(dims)


def stacked_from(value, axes, order):
    pieces = value
    for k in order:
        pieces = lax.all_gather(pieces, axes[k])
    done = order[::-1]
    back = [done.index(k) for k in range(len(axes))]
    pieces = pieces.transpose(*back, *range(len(axes), pieces.ndim))
    return pieces.reshape(-1, *value.shape)


def whole_of(value, axes, order, dim):
    return joined_along(stacked_from(value, axes, order), dim)


def stencil_sum(padded):
    plane = (
        padded[2:, 1:-1, 1:-1]
        + padded[:-2, 1:-1, 1:-1]
        + padded[1:-1, 2:, 1:-1]
        + padded[1:-1, :-2, 1:-1]
    )
    sight = padded[1:-1, 1:-1, 2:] + padded[1:-1, 1:-1, :-2]
    return plane + (1.0 + rsd_beta) * sight


def grid_index(shape, starts):
    return [lax.broadcasted_iota(jnp.int32, shape, which) + starts[which] for which in range(3)]


def parity_of(shape, starts):
    position = grid_index(shape, starts)
    return (position[0] + position[1] + position[2] + 6) % 2


def inside_grid(shape, starts, whole):
    position = grid_index(shape, starts)
    keep = (position[0] >= 0) & (position[0] < whole[0])
    for which in (1, 2):
        keep = keep & (position[which] >= 0) & (position[which] < whole[which])
    return keep


def half_sweep(field, source, scale, chosen):
    update = (source / scale + stencil_sum(jnp.pad(field, 1))) / centre
    return jnp.where(chosen, update, field)


def full_sweep(field, source, scale, parity):
    field = half_sweep(field, source, scale, parity == 0)
    return half_sweep(field, source, scale, parity == 1)


def restrict(residue):
    shape = residue.shape
    blocks = residue.reshape(shape[0] // 2, 2, shape[1] // 2, 2, shape[2] // 2, 2)
    return jnp.mean(blocks, axis=(1, 3, 5))


def prolong(coarse):
    return jnp.repeat(jnp.repeat(jnp.repeat(coarse, 2, 0), 2, 1), 2, 2)


def local_cycle(source, level):
    scale = 0.25**level
    parity = parity_of(source.shape, (0, 0, 0))
    field = jnp.zeros_like(source)
    if level == LEVELS - 1:
        for number in range(CSWEEPS):
            field = full_sweep(field, source, scale, parity)
        return field
    for number in range(2):
        field = full_sweep(field, source, scale, parity)
    residue = source - scale * (centre * field - stencil_sum(jnp.pad(field, 1)))
    field = field + prolong(local_cycle(restrict(residue), level + 1))
    for number in range(2):
        field = full_sweep(field, source, scale, parity)
    return field


def faces(field):
    return with_halo(field, ((GX, 0), ("gy", 1), ("gz", 2)), 1)


def wide(field):
    return extended_2(field, ((GX, 0), ("gy", 1), ("gz", 2)), 2)


def block_starts(shape, margin):
    return (
        lax.axis_index(GX) * shape[0] - margin,
        lax.axis_index("gy") * shape[1] - margin,
        lax.axis_index("gz") * shape[2] - margin,
    )


def padded_half(padded, source, scale, chosen):
    field = padded[1:-1, 1:-1, 1:-1]
    update = (source / scale + stencil_sum(padded)) / centre
    return jnp.where(chosen, update, field)


def wide_sweep(extended, wide_source, scale, red_wide, source, black):
    update = (wide_source / scale + stencil_sum(jnp.pad(extended, 1))) / centre
    extended = jnp.where(red_wide, update, extended)
    return padded_half(extended[1:-1, 1:-1, 1:-1], source, scale, black)


def coarse_level(source, level):
    shape = source.shape
    stack = whole_of(source[None], GX_GY_GZ, (0, 2, 3, 1), 0)
    count_x, count_y, count_z = (lax.axis_size(GX), lax.axis_size("gy"), lax.axis_size("gz"))
    whole = stack.reshape(count_x, count_y, count_z, shape[0], shape[1], shape[2])
    whole = whole.transpose(0, 3, 1, 4, 2, 5).reshape(
        count_x * shape[0], count_y * shape[1], count_z * shape[2]
    )
    solved = local_cycle(whole, level)
    starts = block_starts(shape, 0)
    return lax.dynamic_slice(solved, starts, shape)


def shared_cycle(source, level, top):
    if level == top:
        return coarse_level(source, level)
    scale = 0.25**level
    shape = source.shape
    whole = (
        shape[0] * lax.axis_size(GX),
        shape[1] * lax.axis_size("gy"),
        shape[2] * lax.axis_size("gz"),
    )
    parity = parity_of(shape, block_starts(shape, 0))
    black = parity == 1
    wide_shape = (shape[0] + 4, shape[1] + 4, shape[2] + 4)
    wide_starts = block_starts(shape, 2)
    red_wide = (parity_of(wide_shape, wide_starts) == 0) & inside_grid(
        wide_shape, wide_starts, whole
    )
    wide_source = wide(source)
    field = wide_sweep(
        jnp.zeros(wide_shape, jnp.float32), wide_source, scale, red_wide, source, black
    )
    field = wide_sweep(wide(field), wide_source, scale, red_wide, source, black)
    residue = source - scale * (centre * field - stencil_sum(faces(field)))
    field = field + prolong(shared_cycle(restrict(residue), level + 1, top))
    for number in range(2):
        field = wide_sweep(wide(field), wide_source, scale, red_wide, source, black)
    return field


def on_device(density):
    top = 3
    return shared_cycle(density, 0, top)


def solution(mesh):
    finer = Mesh(
        mesh.devices.reshape(4, 2, mesh.shape["gy"], mesh.shape["gz"]), ("gx_0", "gx_1", "gy", "gz")
    )
    return jax.shard_map(
        on_device,
        mesh=finer,
        in_specs=(P(GX, "gy", "gz"),),
        out_specs=P(GX, "gy", "gz"),
        check_vma=False,
    )
```

profile of v0, /device:TPU:1, one launch (start us, length us, event | category | flops | bytes accessed | tf_op | source)
XLA Modules:
  0.0 521.3 jit_solution(4265817883745202102)
XLA Ops:
  0.7 4.6 collective-permute-start
  10.4 3.5 collective-permute-start.2
  15.3 3.6 collective-permute-done.3
  23.6 8.4 %collective-permute-done.4 = f32[36,20,2]{2,1,0:T(8,128)S(1)} collective-permute-done((f32[36,20,2]{2,1,0:T(8,128)S(1)}, f32[36,20,2]{2,1,0:T(8,128)S(1)}, u32[]{:S(2)}, u32[]{:S(2)}) %collective-permute-start.4) | collective-permute-done | bytes 5792 | tf_op jit(solution)/shard_map/ppermute | solution.py:44
  31.9 4.4 collective-permute-done.5
  40.0 3.5 collective-permute-start.6
  48.6 3.5 collective-permute-start.8
  53.4 4.8 collective-permute-done.9
  62.9 8.3 %collective-permute-done.10 = f32[36,20,2]{2,1,0:T(8,128)S(1)} collective-permute-done((f32[36,20,2]{2,1,0:T(8,128)S(1)}, f32[36,20,2]{2,1,0:T(8,128)S(1)}, u32[]{:S(2)}, u32[]{:S(2)}) %collective-permute-start.10) | collective-permute-done | bytes 5792 | tf_op jit(solution)/shard_map/ppermute | solution.py:44
  71.2 4.3 collective-permute-done.11
  81.5 4.0 collective-permute-start.17
  85.6 5.2 collective-permute-start.15
  98.5 18.1 %reshape.84 = f32[16,2,8,2,64,2]{5,4,3,2,1,0:T(8,128)} reshape(f32[32,16,128]{2,1,0:T(8,128)S(1)} %fusion.110) | data formatting | bytes 524288 | tf_op jit(solution)/shard_map/reshape | solution.py:110
  116.6 7.0 %reduce_sum.54 = f32[16,8,64]{2,1,0:T(8,128)S(1)} reduce(f32[16,2,8,2,64,2]{5,4,3,2,1,0:T(8,128)} %reshape.84, f32[]{:T(128)} %constant.282.clone.1), dimensions={1,3,5}, to_apply=%region_0.1 | reduce | flops 57344 | bytes 294916 | tf_op jit(solution)/shard_map/reduce_sum | solution.py:111
  123.6 4.2 collective-permute-start.18
  132.8 3.6 collective-permute-start.20
  147.6 3.8 collective-permute-done.23
  160.3 4.1 collective-permute-start.26
  174.6 4.4 collective-permute-done.29
  182.4 4.0 collective-permute-start.35
  186.4 4.0 collective-permute-start.33
  199.5 4.1 collective-permute-start.36
  208.7 3.6 collective-permute-start.38
  220.0 3.8 collective-permute-done.41
  224.2 4.3 collective-permute-start.42
  244.8 4.2 collective-permute-done.47
  250.7 4.0 collective-permute-start.51
  262.3 4.0 collective-permute-start.53
  267.6 9.1 %all-gather = f32[16,2,16]{2,1,0:T(2,128)S(1)} all-gather(f32[4,2,16]{2,1,0:T(2,128)S(1)} %copy.501), channel_id=2, replica_groups=mesh['gx_0'=4,'gx_1'=2,'gy'=8,'gz'=4] {'gx_0'}, dimensions={0}, use_global_device_ids=true | all-gather | bytes 2560 | tf_op jit(solution)/shard_map/all_gather | solution.py:59
  276.7 18.8 %all-gather.1 = f32[32,1,4,2,16]{4,2,0,3,1:T(4,128)S(1)} all-gather(f32[4,1,4,2,16]{4,2,0,3,1:T(4,128)S(1)} %bitcast.52), channel_id=3, replica_groups=mesh['gx_0'=4,'gx_1'=2,'gy'=8,'gz'=4] {'gy'}, dimensions={0}, use_global_device_ids=true | all-gather | bytes 18432 | tf_op jit(solution)/shard_map/all_gather | solution.py:59
  295.5 9.9 %all-gather.2 = f32[32,4,1,4,2,16]{5,1,0,4,3,2:T(4,128)S(1)} all-gather(f32[8,4,1,4,2,16]{5,1,0,4,3,2:T(4,128)S(1)} %bitcast.41), channel_id=4, replica_groups=mesh['gx_0'=4,'gx_1'=2,'gy'=8,'gz'=4] {'gz'}, dimensions={0}, use_global_device_ids=true | all-gather | bytes 81920 | tf_op jit(solution)/shard_map/all_gather | solution.py:59
  305.5 14.0 %all-gather.3 = f32[8,8,4,1,4,2,16]{6,1,0,5,4,2,3:T(8,128)S(1)} all-gather(f32[4,8,4,1,4,2,16]{6,1,0,5,4,2,3:T(8,128)S(1)} %bitcast.36), channel_id=5, replica_groups=mesh['gx_0'=4,'gx_1'=2,'gy'=8,'gz'=4] {'gx_1'}, dimensions={0}, use_global_device_ids=true | all-gather | bytes 196608 | tf_op jit(solution)/shard_map/all_gather | solution.py:59
  322.3 10.1 %reshape.88 = f32[16,2,8,2,32,2]{5,4,3,2,1,0:T(8,128)} reshape(f32[32,16,64]{2,1,0:T(8,128)S(1)} %fusion.57) | data formatting | bytes 262144 | tf_op jit(solution)/shard_map/reshape | solution.py:110
  332.3 4.1 reduce_sum.57
  350.4 4.1 collective-permute-start.56
  363.2 3.8 collective-permute-done.59
  367.5 4.3 collective-permute-start.60
  388.1 4.2 collective-permute-done.65
  393.1 4.0 collective-permute-start.66
  402.1 3.6 collective-permute-start.68
  410.3 3.6 collective-permute-start.70
  417.6 3.8 collective-permute-done.71
  444.0 3.8 collective-permute-done.77
  449.5 3.7 collective-permute-start.78
  469.8 8.6 %collective-permute-done.82 = f32[36,20,2]{2,1,0:T(8,128)S(1)} collective-permute-done((f32[36,20,2]{2,1,0:T(8,128)S(1)}, f32[36,20,2]{2,1,0:T(8,128)S(1)}, u32[]{:S(2)}, u32[]{:S(2)}) %collective-permute-start.82) | collective-permute-done | bytes 5792 | tf_op jit(solution)/shard_map/ppermute | solution.py:44
  478.4 3.9 collective-permute-done.83
  504.8 8.6 %collective-permute-done.88 = f32[36,20,2]{2,1,0:T(8,128)S(1)} collective-permute-done((f32[36,20,2]{2,1,0:T(8,128)S(1)}, f32[36,20,2]{2,1,0:T(8,128)S(1)}, u32[]{:S(2)}, u32[]{:S(2)}) %collective-permute-start.88) | collective-permute-done | bytes 5792 | tf_op jit(solution)/shard_map/ppermute | solution.py:44
  513.5 3.9 collective-permute-done.89
  (443 shorter events, 249.2 us)
Async XLA Ops:
  0.7 6.7 %collective-permute-start = (f32[2,16,128]{2,1,0:T(8,128)S(1)}, f32[2,16,128]{2,1,0:T(8,128)S(1)}, u32[]{:S(2)}, u32[]{:S(2)}) collective-permute-start(f32[2,16,128]{2,1,0:T(8,128)S(1)} %get-tuple-element.43), channel_id=1, source_target_pairs={{0,32},{32,64},{64,96},{96,128},{128,160},{160,192},{192,224},{1,3... | collective-permute-start | bytes 49160 | tf_op jit(solution)/shard_map/ppermute | solution.py:44
  19.1 12.8 %collective-permute-start.4 = (f32[36,20,2]{2,1,0:T(8,128)S(1)}, f32[36,20,2]{2,1,0:T(8,128)S(1)}, u32[]{:S(2)}, u32[]{:S(2)}) collective-permute-start(f32[36,20,2]{2,1,0:T(8,128)S(1)} %get-tuple-element.13), channel_id=1, source_target_pairs={{0,1},{1,2},{2,3},{4,5},{5,6},{6,7},{8,9},{9,10},{10,11},{12,13},{... | collective-permute-start | bytes 17288 | tf_op jit(solution)/shard_map/ppermute | solution.py:44
  22.3 14.1 %collective-permute-start.5 = (f32[36,20,2]{2,1,0:T(8,128)S(1)}, f32[36,20,2]{2,1,0:T(8,128)S(1)}, u32[]{:S(2)}, u32[]{:S(2)}) collective-permute-start(f32[36,20,2]{2,1,0:T(8,128)S(1)} %get-tuple-element.14), channel_id=1, source_target_pairs={{1,0},{2,1},{3,2},{5,4},{6,5},{7,6},{9,8},{10,9},{11,10},{13,12},{... | collective-permute-start | bytes 17288 | tf_op jit(solution)/shard_map/ppermute | solution.py:45
  40.0 5.5 %collective-permute-start.6 = (f32[2,16,128]{2,1,0:T(8,128)S(1)}, f32[2,16,128]{2,1,0:T(8,128)S(1)}, u32[]{:S(2)}, u32[]{:S(2)}) collective-permute-start(f32[2,16,128]{2,1,0:T(8,128)S(1)} %get-tuple-element.40), channel_id=1, source_target_pairs={{0,32},{32,64},{64,96},{96,128},{128,160},{160,192},{192,224},{1,3... | collective-permute-start | bytes 49160 | tf_op jit(solution)/shard_map/ppermute | solution.py:44
  52.1 6.1 %collective-permute-start.9 = (f32[36,2,128]{2,1,0:T(2,128)S(1)}, f32[36,2,128]{2,1,0:T(2,128)S(1)}, u32[]{:S(2)}, u32[]{:S(2)}) collective-permute-start(f32[36,2,128]{2,1,0:T(2,128)S(1)} %get-tuple-element.20), channel_id=1, source_target_pairs={{4,0},{8,4},{12,8},{16,12},{20,16},{24,20},{28,24},{5,1},{9,5},{13... | collective-permute-start | bytes 110600 | tf_op jit(solution)/shard_map/ppermute | solution.py:45
  58.5 12.7 %collective-permute-start.10 = (f32[36,20,2]{2,1,0:T(8,128)S(1)}, f32[36,20,2]{2,1,0:T(8,128)S(1)}, u32[]{:S(2)}, u32[]{:S(2)}) collective-permute-start(f32[36,20,2]{2,1,0:T(8,128)S(1)} %get-tuple-element.11), channel_id=1, source_target_pairs={{0,1},{1,2},{2,3},{4,5},{5,6},{6,7},{8,9},{9,10},{10,11},{12,13},{... | collective-permute-start | bytes 17288 | tf_op jit(solution)/shard_map/ppermute | solution.py:44
  61.6 13.9 %collective-permute-start.11 = (f32[36,20,2]{2,1,0:T(8,128)S(1)}, f32[36,20,2]{2,1,0:T(8,128)S(1)}, u32[]{:S(2)}, u32[]{:S(2)}) collective-permute-start(f32[36,20,2]{2,1,0:T(8,128)S(1)} %get-tuple-element.12), channel_id=1, source_target_pairs={{1,0},{2,1},{3,2},{5,4},{6,5},{7,6},{9,8},{10,9},{11,10},{13,12},{... | collective-permute-start | bytes 17288 | tf_op jit(solution)/shard_map/ppermute | solution.py:45
  78.9 15.0 %collective-permute-start.14 = (f32[32,1,128]{2,1,0:T(1,128)S(1)}, f32[32,1,128]{2,1,0:T(1,128)S(1)}, u32[]{:S(2)}, u32[]{:S(2)}) collective-permute-start(f32[32,1,128]{2,1,0:T(1,128)S(1)} %get-tuple-element.39), channel_id=1, source_target_pairs={{4,0},{8,4},{12,8},{16,12},{20,16},{24,20},{28,24},{5,1},{9,5},{13... | collective-permute-start | bytes 49160 | tf_op jit(solution)/shard_map/ppermute | solution.py:26
  80.2 17.2 %collective-permute-start.16 = (f32[32,16,1]{2,1,0:T(8,128)S(1)}, f32[32,16,1]{2,1,0:T(8,128)S(1)}, u32[]{:S(2)}, u32[]{:S(2)}) collective-permute-start(f32[32,16,1]{2,1,0:T(8,128)S(1)} %get-tuple-element.34), channel_id=1, source_target_pairs={{1,0},{2,1},{3,2},{5,4},{6,5},{7,6},{9,8},{10,9},{11,10},{13,12},{... | collective-permute-start | bytes 6152 | tf_op jit(solution)/shard_map/ppermute | solution.py:26
  81.5 15.9 %collective-permute-start.17 = (f32[32,16,1]{2,1,0:T(8,128)S(1)}, f32[32,16,1]{2,1,0:T(8,128)S(1)}, u32[]{:S(2)}, u32[]{:S(2)}) collective-permute-start(f32[32,16,1]{2,1,0:T(8,128)S(1)} %get-tuple-element.35), channel_id=1, source_target_pairs={{0,1},{1,2},{2,3},{4,5},{5,6},{6,7},{8,9},{9,10},{10,11},{12,13},{... | collective-permute-start | bytes 6152 | tf_op jit(solution)/shard_map/ppermute | solution.py:25
  85.6 11.8 %collective-permute-start.15 = (f32[32,1,128]{2,1,0:T(1,128)S(1)}, f32[32,1,128]{2,1,0:T(1,128)S(1)}, u32[]{:S(2)}, u32[]{:S(2)}) collective-permute-start(f32[32,1,128]{2,1,0:T(1,128)S(1)} %get-tuple-element.38), channel_id=1, source_target_pairs={{0,4},{4,8},{8,12},{12,16},{16,20},{20,24},{24,28},{1,5},{5,9},{9,... | collective-permute-start | bytes 49160 | tf_op jit(solution)/shard_map/ppermute | solution.py:25
  90.8 6.7 %collective-permute-start.12 = (f32[1,16,128]{2,1,0:T(8,128)S(1)}, f32[1,16,128]{2,1,0:T(8,128)S(1)}, u32[]{:S(2)}, u32[]{:S(2)}) collective-permute-start(f32[1,16,128]{2,1,0:T(8,128)S(1)} %get-tuple-element.37), channel_id=1, source_target_pairs={{32,0},{64,32},{96,64},{128,96},{160,128},{192,160},{224,192},{33,... | collective-permute-start | bytes 24584 | tf_op jit(solution)/shard_map/ppermute | solution.py:26
  123.6 6.2 %collective-permute-start.18 = (f32[2,8,64]{2,1,0:T(8,128)S(1)}, f32[2,8,64]{2,1,0:T(8,128)S(1)}, u32[]{:S(2)}, u32[]{:S(2)}) collective-permute-start(f32[2,8,64]{2,1,0:T(8,128)S(1)} %get-tuple-element.72), channel_id=1, source_target_pairs={{0,32},{32,64},{64,96},{96,128},{128,160},{160,192},{192,224},{1,3... | collective-permute-start | bytes 12296 | tf_op jit(solution)/shard_map/ppermute | solution.py:44
  141.1 6.4 %collective-permute-start.22 = (f32[20,12,2]{2,0,1:T(8,128)S(1)}, f32[20,12,2]{2,0,1:T(8,128)S(1)}, u32[]{:S(2)}, u32[]{:S(2)}) collective-permute-start(f32[20,12,2]{2,0,1:T(8,128)S(1)} %get-tuple-element.50), channel_id=1, source_target_pairs={{0,1},{1,2},{2,3},{4,5},{5,6},{6,7},{8,9},{9,10},{10,11},{12,13},{... | collective-permute-start | bytes 5768 | tf_op jit(solution)/shard_map/ppermute | solution.py:44
  143.9 7.5 %collective-permute-start.23 = (f32[20,12,2]{2,0,1:T(8,128)S(1)}, f32[20,12,2]{2,0,1:T(8,128)S(1)}, u32[]{:S(2)}, u32[]{:S(2)}) collective-permute-start(f32[20,12,2]{2,0,1:T(8,128)S(1)} %get-tuple-element.51), channel_id=1, source_target_pairs={{1,0},{2,1},{3,2},{5,4},{6,5},{7,6},{9,8},{10,9},{11,10},{13,12},{... | collective-permute-start | bytes 5768 | tf_op jit(solution)/shard_map/ppermute | solution.py:45
  152.1 5.2 collective-permute-start.24
  160.3 5.4 %collective-permute-start.26 = (f32[20,2,64]{2,1,0:T(2,128)S(1)}, f32[20,2,64]{2,1,0:T(2,128)S(1)}, u32[]{:S(2)}, u32[]{:S(2)}) collective-permute-start(f32[20,2,64]{2,1,0:T(2,128)S(1)} %get-tuple-element.57), channel_id=1, source_target_pairs={{0,4},{4,8},{8,12},{12,16},{16,20},{20,24},{24,28},{1,5},{5,9},{9,... | collective-permute-start | bytes 30728 | tf_op jit(solution)/shard_map/ppermute | solution.py:44
  169.3 5.3 %collective-permute-start.28 = (f32[20,12,2]{2,0,1:T(8,128)S(1)}, f32[20,12,2]{2,0,1:T(8,128)S(1)}, u32[]{:S(2)}, u32[]{:S(2)}) collective-permute-start(f32[20,12,2]{2,0,1:T(8,128)S(1)} %get-tuple-element.48), channel_id=1, source_target_pairs={{0,1},{1,2},{2,3},{4,5},{5,6},{6,7},{8,9},{9,10},{10,11},{12,13},{... | collective-permute-start | bytes 5768 | tf_op jit(solution)/shard_map/ppermute | solution.py:44
  171.3 7.8 %collective-permute-start.29 = (f32[20,12,2]{2,0,1:T(8,128)S(1)}, f32[20,12,2]{2,0,1:T(8,128)S(1)}, u32[]{:S(2)}, u32[]{:S(2)}) collective-permute-start(f32[20,12,2]{2,0,1:T(8,128)S(1)} %get-tuple-element.49), channel_id=1, source_target_pairs={{1,0},{2,1},{3,2},{5,4},{6,5},{7,6},{9,8},{10,9},{11,10},{13,12},{... | collective-permute-start | bytes 5768 | tf_op jit(solution)/shard_map/ppermute | solution.py:45
  179.8 14.0 %collective-permute-start.32 = (f32[16,1,64]{2,1,0:T(1,128)S(1)}, f32[16,1,64]{2,1,0:T(1,128)S(1)}, u32[]{:S(2)}, u32[]{:S(2)}) collective-permute-start(f32[16,1,64]{2,1,0:T(1,128)S(1)} %get-tuple-element.69), channel_id=1, source_target_pairs={{4,0},{8,4},{12,8},{16,12},{20,16},{24,20},{28,24},{5,1},{9,5},{13... | collective-permute-start | bytes 12296 | tf_op jit(solution)/shard_map/ppermute | solution.py:26
  181.1 15.3 %collective-permute-start.34 = (f32[16,8,1]{2,1,0:T(8,128)S(1)}, f32[16,8,1]{2,1,0:T(8,128)S(1)}, u32[]{:S(2)}, u32[]{:S(2)}) collective-permute-start(f32[16,8,1]{2,1,0:T(8,128)S(1)} %get-tuple-element.64), channel_id=1, source_target_pairs={{1,0},{2,1},{3,2},{5,4},{6,5},{7,6},{9,8},{10,9},{11,10},{13,12},{... | collective-permute-start | bytes 1544 | tf_op jit(solution)/shard_map/ppermute | solution.py:26
  182.4 14.0 %collective-permute-start.35 = (f32[16,8,1]{2,1,0:T(8,128)S(1)}, f32[16,8,1]{2,1,0:T(8,128)S(1)}, u32[]{:S(2)}, u32[]{:S(2)}) collective-permute-start(f32[16,8,1]{2,1,0:T(8,128)S(1)} %get-tuple-element.65), channel_id=1, source_target_pairs={{0,1},{1,2},{2,3},{4,5},{5,6},{6,7},{8,9},{9,10},{10,11},{12,13},{... | collective-permute-start | bytes 1544 | tf_op jit(solution)/shard_map/ppermute | solution.py:25
  186.4 9.9 %collective-permute-start.33 = (f32[16,1,64]{2,1,0:T(1,128)S(1)}, f32[16,1,64]{2,1,0:T(1,128)S(1)}, u32[]{:S(2)}, u32[]{:S(2)}) collective-permute-start(f32[16,1,64]{2,1,0:T(1,128)S(1)} %get-tuple-element.68), channel_id=1, source_target_pairs={{0,4},{4,8},{8,12},{12,16},{16,20},{20,24},{24,28},{1,5},{5,9},{9,... | collective-permute-start | bytes 12296 | tf_op jit(solution)/shard_map/ppermute | solution.py:25
  190.4 6.0 %collective-permute-start.30 = (f32[1,8,64]{2,1,0:T(8,128)S(1)}, f32[1,8,64]{2,1,0:T(8,128)S(1)}, u32[]{:S(2)}, u32[]{:S(2)}) collective-permute-start(f32[1,8,64]{2,1,0:T(8,128)S(1)} %get-tuple-element.67), channel_id=1, source_target_pairs={{32,0},{64,32},{96,64},{128,96},{160,128},{192,160},{224,192},{33,... | collective-permute-start | bytes 6152 | tf_op jit(solution)/shard_map/ppermute | solution.py:26
  199.5 6.1 %collective-permute-start.36 = (f32[2,4,32]{2,1,0:T(4,128)S(1)}, f32[2,4,32]{2,1,0:T(4,128)S(1)}, u32[]{:S(2)}, u32[]{:S(2)}) collective-permute-start(f32[2,4,32]{2,1,0:T(4,128)S(1)} %get-tuple-element.102), channel_id=1, source_target_pairs={{0,32},{32,64},{64,96},{96,128},{128,160},{160,192},{192,224},{1,3... | collective-permute-start | bytes 3080 | tf_op jit(solution)/shard_map/ppermute | solution.py:44
  218.5 5.3 %collective-permute-start.41 = (f32[12,8,2]{2,1,0:T(8,128)S(1)}, f32[12,8,2]{2,1,0:T(8,128)S(1)}, u32[]{:S(2)}, u32[]{:S(2)}) collective-permute-start(f32[12,8,2]{2,1,0:T(8,128)S(1)} %get-tuple-element.81), channel_id=1, source_target_pairs={{1,0},{2,1},{3,2},{5,4},{6,5},{7,6},{9,8},{10,9},{11,10},{13,12},{... | collective-permute-start | bytes 2312 | tf_op jit(solution)/shard_map/ppermute | solution.py:45
  224.2 6.2 %collective-permute-start.42 = (f32[2,4,32]{2,1,0:T(4,128)S(1)}, f32[2,4,32]{2,1,0:T(4,128)S(1)}, u32[]{:S(2)}, u32[]{:S(2)}) collective-permute-start(f32[2,4,32]{2,1,0:T(4,128)S(1)} %get-tuple-element.100), channel_id=1, source_target_pairs={{0,32},{32,64},{64,96},{96,128},{128,160},{160,192},{192,224},{1,3... | collective-permute-start | bytes 3080 | tf_op jit(solution)/shard_map/ppermute | solution.py:44
  243.3 5.6 %collective-permute-start.47 = (f32[12,8,2]{2,1,0:T(8,128)S(1)}, f32[12,8,2]{2,1,0:T(8,128)S(1)}, u32[]{:S(2)}, u32[]{:S(2)}) collective-permute-start(f32[12,8,2]{2,1,0:T(8,128)S(1)} %get-tuple-element.79), channel_id=1, source_target_pairs={{1,0},{2,1},{3,2},{5,4},{6,5},{7,6},{9,8},{10,9},{11,10},{13,12},{... | collective-permute-start | bytes 2312 | tf_op jit(solution)/shard_map/ppermute | solution.py:45
  249.4 12.8 %collective-permute-start.50 = (f32[8,1,32]{2,1,0:T(1,128)S(1)}, f32[8,1,32]{2,1,0:T(1,128)S(1)}, u32[]{:S(2)}, u32[]{:S(2)}) collective-permute-start(f32[8,1,32]{2,1,0:T(1,128)S(1)} %get-tuple-element.99), channel_id=1, source_target_pairs={{4,0},{8,4},{12,8},{16,12},{20,16},{24,20},{28,24},{5,1},{9,5},{13... | collective-permute-start | bytes 3080 | tf_op jit(solution)/shard_map/ppermute | solution.py:26
  250.7 15.6 %collective-permute-start.51 = (f32[8,1,32]{2,1,0:T(1,128)S(1)}, f32[8,1,32]{2,1,0:T(1,128)S(1)}, u32[]{:S(2)}, u32[]{:S(2)}) collective-permute-start(f32[8,1,32]{2,1,0:T(1,128)S(1)} %get-tuple-element.98), channel_id=1, source_target_pairs={{0,4},{4,8},{8,12},{12,16},{16,20},{20,24},{24,28},{1,5},{5,9},{9,... | collective-permute-start | bytes 3080 | tf_op jit(solution)/shard_map/ppermute | solution.py:25
  254.7 12.4 %collective-permute-start.48 = (f32[1,4,32]{2,1,0:T(4,128)S(1)}, f32[1,4,32]{2,1,0:T(4,128)S(1)}, u32[]{:S(2)}, u32[]{:S(2)}) collective-permute-start(f32[1,4,32]{2,1,0:T(4,128)S(1)} %get-tuple-element.97), channel_id=1, source_target_pairs={{32,0},{64,32},{96,64},{128,96},{160,128},{192,160},{224,192},{33,... | collective-permute-start | bytes 1544 | tf_op jit(solution)/shard_map/ppermute | solution.py:26
  257.7 9.5 %collective-permute-start.49 = (f32[1,4,32]{2,1,0:T(4,128)S(1)}, f32[1,4,32]{2,1,0:T(4,128)S(1)}, u32[]{:S(2)}, u32[]{:S(2)}) collective-permute-start(f32[1,4,32]{2,1,0:T(4,128)S(1)} %get-tuple-element.96), channel_id=1, source_target_pairs={{0,32},{32,64},{64,96},{96,128},{128,160},{160,192},{192,224},{1,3... | collective-permute-start | bytes 1544 | tf_op jit(solution)/shard_map/ppermute | solution.py:25
  261.0 5.3 %collective-permute-start.52 = (f32[8,4,1]{2,1,0:T(4,128)S(1)}, f32[8,4,1]{2,1,0:T(4,128)S(1)}, u32[]{:S(2)}, u32[]{:S(2)}) collective-permute-start(f32[8,4,1]{2,1,0:T(4,128)S(1)} %get-tuple-element.94), channel_id=1, source_target_pairs={{1,0},{2,1},{3,2},{5,4},{6,5},{7,6},{9,8},{10,9},{11,10},{13,12},{... | collective-permute-start | bytes 392 | tf_op jit(solution)/shard_map/ppermute | solution.py:26
  350.4 5.4 %collective-permute-start.56 = (f32[12,2,32]{2,1,0:T(2,128)S(1)}, f32[12,2,32]{2,1,0:T(2,128)S(1)}, u32[]{:S(2)}, u32[]{:S(2)}) collective-permute-start(f32[12,2,32]{2,1,0:T(2,128)S(1)} %get-tuple-element.84), channel_id=1, source_target_pairs={{0,4},{4,8},{8,12},{12,16},{16,20},{20,24},{24,28},{1,5},{5,9},{9,... | collective-permute-start | bytes 9224 | tf_op jit(solution)/shard_map/ppermute | solution.py:44
  361.7 5.3 %collective-permute-start.59 = (f32[12,8,2]{2,1,0:T(8,128)S(1)}, f32[12,8,2]{2,1,0:T(8,128)S(1)}, u32[]{:S(2)}, u32[]{:S(2)}) collective-permute-start(f32[12,8,2]{2,1,0:T(8,128)S(1)} %get-tuple-element.77), channel_id=1, source_target_pairs={{1,0},{2,1},{3,2},{5,4},{6,5},{7,6},{9,8},{10,9},{11,10},{13,12},{... | collective-permute-start | bytes 2312 | tf_op jit(solution)/shard_map/ppermute | solution.py:45
  367.5 6.2 %collective-permute-start.60 = (f32[2,4,32]{2,1,0:T(4,128)S(1)}, f32[2,4,32]{2,1,0:T(4,128)S(1)}, u32[]{:S(2)}, u32[]{:S(2)}) collective-permute-start(f32[2,4,32]{2,1,0:T(4,128)S(1)} %get-tuple-element.90), channel_id=1, source_target_pairs={{0,32},{32,64},{64,96},{96,128},{128,160},{160,192},{192,224},{1,3... | collective-permute-start | bytes 3080 | tf_op jit(solution)/shard_map/ppermute | solution.py:44
  386.7 5.6 %collective-permute-start.65 = (f32[12,8,2]{2,1,0:T(8,128)S(1)}, f32[12,8,2]{2,1,0:T(8,128)S(1)}, u32[]{:S(2)}, u32[]{:S(2)}) collective-permute-start(f32[12,8,2]{2,1,0:T(8,128)S(1)} %get-tuple-element.75), channel_id=1, source_target_pairs={{1,0},{2,1},{3,2},{5,4},{6,5},{7,6},{9,8},{10,9},{11,10},{13,12},{... | collective-permute-start | bytes 2312 | tf_op jit(solution)/shard_map/ppermute | solution.py:45
  393.1 5.9 %collective-permute-start.66 = (f32[2,8,64]{2,1,0:T(8,128)S(1)}, f32[2,8,64]{2,1,0:T(8,128)S(1)}, u32[]{:S(2)}, u32[]{:S(2)}) collective-permute-start(f32[2,8,64]{2,1,0:T(8,128)S(1)} %get-tuple-element.62), channel_id=1, source_target_pairs={{0,32},{32,64},{64,96},{96,128},{128,160},{160,192},{192,224},{1,3... | collective-permute-start | bytes 12296 | tf_op jit(solution)/shard_map/ppermute | solution.py:44
  410.3 7.3 %collective-permute-start.70 = (f32[20,12,2]{2,0,1:T(8,128)S(1)}, f32[20,12,2]{2,0,1:T(8,128)S(1)}, u32[]{:S(2)}, u32[]{:S(2)}) collective-permute-start(f32[20,12,2]{2,0,1:T(8,128)S(1)} %get-tuple-element.46), channel_id=1, source_target_pairs={{0,1},{1,2},{2,3},{4,5},{5,6},{6,7},{8,9},{9,10},{10,11},{12,13},{... | collective-permute-start | bytes 5768 | tf_op jit(solution)/shard_map/ppermute | solution.py:44
  413.9 7.5 %collective-permute-start.71 = (f32[20,12,2]{2,0,1:T(8,128)S(1)}, f32[20,12,2]{2,0,1:T(8,128)S(1)}, u32[]{:S(2)}, u32[]{:S(2)}) collective-permute-start(f32[20,12,2]{2,0,1:T(8,128)S(1)} %get-tuple-element.47), channel_id=1, source_target_pairs={{1,0},{2,1},{3,2},{5,4},{6,5},{7,6},{9,8},{10,9},{11,10},{13,12},{... | collective-permute-start | bytes 5768 | tf_op jit(solution)/shard_map/ppermute | solution.py:45
  422.2 5.1 collective-permute-start.72
  438.4 5.6 %collective-permute-start.76 = (f32[20,12,2]{2,0,1:T(8,128)S(1)}, f32[20,12,2]{2,0,1:T(8,128)S(1)}, u32[]{:S(2)}, u32[]{:S(2)}) collective-permute-start(f32[20,12,2]{2,0,1:T(8,128)S(1)} %get-tuple-element.44), channel_id=1, source_target_pairs={{0,1},{1,2},{2,3},{4,5},{5,6},{6,7},{8,9},{9,10},{10,11},{12,13},{... | collective-permute-start | bytes 5768 | tf_op jit(solution)/shard_map/ppermute | solution.py:44
  440.3 7.5 %collective-permute-start.77 = (f32[20,12,2]{2,0,1:T(8,128)S(1)}, f32[20,12,2]{2,0,1:T(8,128)S(1)}, u32[]{:S(2)}, u32[]{:S(2)}) collective-permute-start(f32[20,12,2]{2,0,1:T(8,128)S(1)} %get-tuple-element.45), channel_id=1, source_target_pairs={{1,0},{2,1},{3,2},{5,4},{6,5},{7,6},{9,8},{10,9},{11,10},{13,12},{... | collective-permute-start | bytes 5768 | tf_op jit(solution)/shard_map/ppermute | solution.py:45
  449.5 5.6 %collective-permute-start.78 = (f32[2,16,128]{2,1,0:T(8,128)S(1)}, f32[2,16,128]{2,1,0:T(8,128)S(1)}, u32[]{:S(2)}, u32[]{:S(2)}) collective-permute-start(f32[2,16,128]{2,1,0:T(8,128)S(1)} %get-tuple-element.25), channel_id=1, source_target_pairs={{0,32},{32,64},{64,96},{96,128},{128,160},{160,192},{192,224},{1,3... | collective-permute-start | bytes 49160 | tf_op jit(solution)/shard_map/ppermute | solution.py:44
  466.5 11.9 %collective-permute-start.82 = (f32[36,20,2]{2,1,0:T(8,128)S(1)}, f32[36,20,2]{2,1,0:T(8,128)S(1)}, u32[]{:S(2)}, u32[]{:S(2)}) collective-permute-start(f32[36,20,2]{2,1,0:T(8,128)S(1)} %get-tuple-element.9), channel_id=1, source_target_pairs={{0,1},{1,2},{2,3},{4,5},{5,6},{6,7},{8,9},{9,10},{10,11},{12,13},{... | collective-permute-start | bytes 17288 | tf_op jit(solution)/shard_map/ppermute | solution.py:44
  468.5 13.9 %collective-permute-start.83 = (f32[36,20,2]{2,1,0:T(8,128)S(1)}, f32[36,20,2]{2,1,0:T(8,128)S(1)}, u32[]{:S(2)}, u32[]{:S(2)}) collective-permute-start(f32[36,20,2]{2,1,0:T(8,128)S(1)} %get-tuple-element.10), channel_id=1, source_target_pairs={{1,0},{2,1},{3,2},{5,4},{6,5},{7,6},{9,8},{10,9},{11,10},{13,12},{... | collective-permute-start | bytes 17288 | tf_op jit(solution)/shard_map/ppermute | solution.py:45
  501.6 11.9 %collective-permute-start.88 = (f32[36,20,2]{2,1,0:T(8,128)S(1)}, f32[36,20,2]{2,1,0:T(8,128)S(1)}, u32[]{:S(2)}, u32[]{:S(2)}) collective-permute-start(f32[36,20,2]{2,1,0:T(8,128)S(1)} %get-tuple-element.7), channel_id=1, source_target_pairs={{0,1},{1,2},{2,3},{4,5},{5,6},{6,7},{8,9},{9,10},{10,11},{12,13},{... | collective-permute-start | bytes 17288 | tf_op jit(solution)/shard_map/ppermute | solution.py:44
  503.5 13.9 %collective-permute-start.89 = (f32[36,20,2]{2,1,0:T(8,128)S(1)}, f32[36,20,2]{2,1,0:T(8,128)S(1)}, u32[]{:S(2)}, u32[]{:S(2)}) collective-permute-start(f32[36,20,2]{2,1,0:T(8,128)S(1)} %get-tuple-element.8), channel_id=1, source_target_pairs={{1,0},{2,1},{3,2},{5,4},{6,5},{7,6},{9,8},{10,9},{11,10},{13,12},{... | collective-permute-start | bytes 17288 | tf_op jit(solution)/shard_map/ppermute | solution.py:45
  (67 other events, 2199.0 us)
where the time goes:
time: 524 us; the launch traced here: 521 us
  starting transfers between devices  221 us (42%)
  waiting for transfers between devices  170 us (32%)
  blocking collectives  51.8 us (10%)
  local copies, waits for them, and re-layouts  39.1 us (7%)
  other arithmetic  36.1 us (7%)
    ppermute x36, waiting for transfers between devices, extended_2(): after = lax.ppermute(leading, axis, down)  125 us
    ppermute x36, starting transfers between devices, extended_2(): before = lax.ppermute(last, axis, up)  115 us
    ppermute x36, starting transfers between devices, extended_2(): after = lax.ppermute(leading, axis, down)  54.3 us
    all_gather x4, blocking collectives, stacked_from(): pieces = lax.all_gather(pieces, axes[k])  51.8 us
    ppermute x36, waiting for transfers between devices, extended_2(): before = lax.ppermute(last, axis, up)  43.3 us
    ppermute x9, starting transfers between devices, with_halo(): lax.ppermute(last, axis, up)  34.3 us
    reshape x6, local copies, waits for them, and re-layouts, restrict(): residue.reshape(shape[0] // 2, 2, shape[1] // 2, 2, shape[2] // 2, 2)  31.1 us
    ppermute x9, starting transfers between devices, with_halo(): lax.ppermute(leading, axis, [(b, a) for a, b in up])  17.2 us
  transfers between devices with their start and end apart: 90, of which 50 were waited for; matrix products, arithmetic and copies ran while one was open for 0% of the time, Pallas kernels for 0%

commit v1 on v0

v1 whole, which is shorter than its diff:
```python
import itertools

import jax
import jax.numpy as jnp
from jax import lax
from jax.experimental import pallas as pl
from jax.experimental.pallas import tpu as pltpu
from jax.sharding import PartitionSpec as P

MESH = pl.DeviceIdType.MESH
F32 = jnp.float32
HIGHEST = lax.Precision.HIGHEST

NGX, NGY, NGZ = 8, 8, 4
BX, BY, BZ = 32, 16, 128
CSWEEPS = 4
BETA1 = 1.5
INV = 1.0 / (4.0 + 2.0 * BETA1)

D26 = [d for d in itertools.product((-1, 0, 1), repeat=3) if d != (0, 0, 0)]
D44 = [d for d in itertools.product((-1, 0, 1), (-2, -1, 0, 1, 2), (-1, 0, 1)) if d != (0, 0, 0)]
XY4 = [(-1, -1), (-1, 1), (1, -1), (1, 1)]
Z18 = [d for d in D26 if d[2] != 0]


def roll(x, shift, axis):
    size = x.shape[axis]
    shift = shift % size
    return x if shift == 0 else pltpu.roll(x, shift, axis)


def iota(shape, dim):
    return lax.broadcasted_iota(jnp.int32, shape, dim)


def both(cond, a, b):
    return jnp.where(cond, a, b)


def side(n):
    return 0 if n < 0 else 1


def kernel(
    f_hbm, out_hbm,
    fm, fh, vm, vh, mm, mh, s0, pe0m, pe0h, tmp0,
    g1, v1, m1, s1, pe1, tmp1,
    g2, v2, m2, s2, pe2, tmp2,
    fy0, fz0, vy0, vz0, fk1, fz1, vk1, vz1, ft2, vt2,
    fx_r, fy_r, fxy_r, fz_r, vx_r, vy_r, vxy_r, vz_r,
    f1x_r, f1y_r, f1xy_r, f1z_r, v1x_r, v1y_r, v1xy_r, v1z_r,
    f2_r, v2_r,
    t3, gy_r, gzb, gxb, g3, v3,
    io_sem, s_f0, r_f0, s_v0, r_v0, s_f1, r_f1, s_v1, r_v1, s_f2, r_f2, s_v2, r_v2, s_g, r_g,
):
    ix, iy, iz = lax.axis_index("gx"), lax.axis_index("gy"), lax.axis_index("gz")

    def there(n):
        nx, ny, nz = ix + n[0], iy + n[1], iz + n[2]
        return (nx >= 0) & (nx < NGX) & (ny >= 0) & (ny < NGY) & (nz >= 0) & (nz < NGZ)

    def at(n):
        return (
            jnp.clip(ix + n[0], 0, NGX - 1),
            jnp.clip(iy + n[1], 0, NGY - 1),
            jnp.clip(iz + n[2], 0, NGZ - 1),
        )

    def neg(n):
        return (-n[0], -n[1], -n[2])

    load = pltpu.make_async_copy(f_hbm, fm.at[pl.ds(4, BX), pl.ds(8, BY), :], io_sem.at[0])
    load.start()

    barrier = pltpu.get_barrier_semaphore()
    count = 0
    for d in D44:
        ok = there(d)
        count = count + ok.astype(jnp.int32)

        @pl.when(ok)
        def _(d=d):
            pl.semaphore_signal(barrier, inc=1, device_id=at(d), device_id_type=MESH)

    lines = []
    for k in range(1, NGY):
        lines.append((ix, lax.rem(iy + k, NGY), iz))
    for k in range(1, NGZ):
        lines.append((ix, iy, lax.rem(iz + k, NGZ)))
    for k in range(1, NGX):
        lines.append((lax.rem(ix + k, NGX), iy, iz))
    for peer in lines:
        pl.semaphore_signal(barrier, inc=1, device_id=peer, device_id_type=MESH)

    lane = iota((8, 128), 1)
    row = iota((8, 128), 0)

    def fill_masks(ref, rows, lanes_pos, lanes_ok, rows_pos, rows_ok):
        ok = rows_ok & lanes_ok
        par = (rows_pos + lanes_pos) & 1
        ref[0] = jnp.where(ok & (par == 0), 1.0, 0.0)
        ref[1] = jnp.where(ok & (par == 1), 1.0, 0.0)
        ref[2] = jnp.zeros((24, 128), F32)
        ref[3] = jnp.where(ok, 1.0, 0.0)

    r24, l24 = iota((24, 128), 0), iota((24, 128), 1)
    y0 = iy * BY + r24 - 4
    oky0 = (y0 >= 0) & (y0 < NGY * BY)
    z0 = iz * BZ + l24
    fill_masks(mm, 24, z0, z0 >= 0, y0, oky0)
    z0h = iz * BZ + l24 + jnp.where(l24 < 64, 128, -128)
    fill_masks(mh, 24, z0h, (z0h >= 0) & (z0h < NGZ * BZ) & ((l24 < 4) | (l24 >= 124)), y0, oky0)
    y1 = iy * 8 + r24 - 8
    z1 = iz * 64 + l24 - 6
    fill_masks(m1, 24, z1, (z1 >= 0) & (z1 < NGZ * 64) & (l24 < 76), y1, (y1 >= 0) & (y1 < NGY * 8))
    x2 = ix * 8 + r24 - 8
    z2 = iz * 32 + l24 - 7
    fill_masks(m2, 24, z2, (z2 >= 0) & (z2 < NGZ * 32) & (l24 < 46), x2, (x2 >= 0) & (x2 < NGX * 8))

    def pick(start, i, total, colour):
        pos = start + i
        return jnp.where((pos >= 0) & (pos < total), (pos + colour + 64) & 1, 2)

    def picked(start, i, total):
        pos = start + i
        return jnp.where((pos >= 0) & (pos < total), 3, 2)

    base0, base1, base2 = ix * BX - 4, ix * 16 - 6, iy * 4 - 7

    for ref in (vm, vh, v1, g1, v2, g2):
        n = ref.shape[0]

        @pl.loop(0, n)
        def _(i, ref=ref):
            ref[i] = jnp.zeros(ref.shape[1:], F32)

    @pl.loop(0, 40)
    def _(i):
        v3[i] = jnp.zeros((8, 128), F32)

    load.wait()

    def pack0(src, yp, zp):
        def ypack(t, c):
            yp[0, t] = jnp.concatenate([src[4 + 2 * t, 8:12, :], src[5 + 2 * t, 8:12, :]], axis=0)
            yp[1, t] = jnp.concatenate([src[4 + 2 * t, 20:24, :], src[5 + 2 * t, 20:24, :]], axis=0)
            return c

        lax.fori_loop(0, 16, ypack, 0, unroll=4)
        lane16 = iota((16, 128), 1)
        lo = jnp.zeros((16, 128), F32)
        hi = jnp.zeros((16, 128), F32)
        for x in range(BX):
            p = roll(src[4 + x, 8:24, :], 4 * x, 1)
            lo = jnp.where(lane16 // 4 == x, p, lo)
            hi = jnp.where(lane16 // 4 == (x - 1) % BX, p, hi)
        zp[0] = lo
        zp[1] = hi

    def copies0(src, yp, zp, xr, yr, xyr, zr, ss, rs, directions):
        out = []
        for d in directions:
            k = D26.index(d)
            dx, dy, dz = d
            nx, ny = -dx, -dy
            if dz == 0 and dy == 0:
                s = src.at[pl.ds(4 if dx < 0 else 32, 4), pl.ds(8, BY), :]
                t = xr.at[side(nx)]
            elif dz == 0 and dx == 0:
                s, t = yp.at[side(dy)], yr.at[side(ny)]
            elif dz == 0:
                s = yp.at[side(dy), pl.ds(0 if dx < 0 else 14, 2)]
                t = xyr.at[XY4.index((nx, ny))]
            else:
                slot = Z18.index(neg(d))
                if dy == 0:
                    s, t = zp.at[side(dz)], zr.at[slot]
                else:
                    rows = pl.ds(0 if dy < 0 else 8, 8)
                    s, t = zp.at[side(dz), rows], zr.at[slot, rows]
            out.append((d, pltpu.make_async_remote_copy(s, t, ss.at[k], rs.at[k], at(d), MESH)))
        return out

    def start(copies):
        for d, c in copies:
            @pl.when(there(d))
            def _(c=c):
                c.start()

    def arrive(copies):
        for d, c in copies:
            @pl.when(there(neg(d)))
            def _(c=c):
                c.wait_recv()

    def sent(copies):
        for d, c in copies:
            @pl.when(there(d))
            def _(c=c):
                c.wait_send()

    def unpack0(main, halo, xr, yr, xyr, zr):
        def faces(x, c):
            main[x, 8:24, :] = xr[0, x]
            main[36 + x, 8:24, :] = xr[1, x]
            return c

        lax.fori_loop(0, 4, faces, 0, unroll=True)

        def yfaces(t, c):
            for ny, rows in ((0, 4), (1, 24)):
                main[4 + 2 * t, rows : rows + 4, :] = yr[ny, t, 0:4, :]
                main[5 + 2 * t, rows : rows + 4, :] = yr[ny, t, 4:8, :]
            return c

        lax.fori_loop(0, 16, yfaces, 0, unroll=4)
        for k, (nx, ny) in enumerate(XY4):
            x0 = 0 if nx < 0 else 36
            rows = 4 if ny < 0 else 24
            for t in range(2):
                main[x0 + 2 * t, rows : rows + 4, :] = xyr[k, t, 0:4, :]
                main[x0 + 2 * t + 1, rows : rows + 4, :] = xyr[k, t, 4:8, :]
        for xe in range(40):
            nx, x = (-1, 28 + xe) if xe < 4 else ((0, xe - 4) if xe < 36 else (1, xe - 36))
            for ny, src, dst, num in ((-1, 8, 0, 8), (0, 0, 8, 16), (1, 0, 24, 8)):
                low = zr[Z18.index((nx, ny, -1)), src : src + num, :]
                high = zr[Z18.index((nx, ny, 1)), src : src + num, :]
                low = roll(low, 124 - 4 * ((x - 1) % BX), 1)
                high = roll(high, -4 * x, 1)
                halo[xe, dst : dst + num, :] = jnp.where(iota((num, 128), 1) < 64, high, low)

    ef0 = copies0(fm, fy0, fz0, fx_r, fy_r, fxy_r, fz_r, s_f0, r_f0, D26)
    ev0 = copies0(vm, vy0, vz0, vx_r, vy_r, vxy_r, vz_r, s_v0, r_v0, D26)

    pack0(fm, fy0, fz0)
    pl.semaphore_wait(barrier, count + len(lines))
    start(ef0)

    l24b = iota((24, 128), 1)

    def planes0(lo, hi, body, step=2):
        def run(i, c):
            body(lo + i * step)
            return c

        lax.fori_loop(0, (hi - lo) // step, run, 0)

    def shifted(c, h):
        lanes = iota(c.shape, 1)
        cr, hr = roll(c, 1, 1), roll(h, 1, 1)
        cl, hl = roll(c, -1, 1), roll(h, -1, 1)
        zm = jnp.where(lanes == 0, hr, cr) + jnp.where(lanes == 127, hl, cl)
        zh = jnp.where(lanes == 0, cr, hr) + jnp.where(lanes == 127, cl, hl)
        return BETA1 * zm, BETA1 * zh

    def half0(lo, hi, colour, last=False):
        def body(x):
            done = []
            for u in range(2):
                i = x + u
                sel = pick(base0, i, NGX * BX, colour)
                if last:
                    c, h = vm[i, 8:24, :], vh[i, 8:24, :]
                    zm, _ = shifted(c, h)
                    s = vm[i - 1, 8:24, :] + vm[i + 1, 8:24, :] + vm[i, 7:23, :] + vm[i, 9:25, :] + zm
                    m = mm[sel, 4:20, :] > 0.5
                    done.append((jnp.where(m, (fm[i, 8:24, :] + s) * INV, c),))
                    continue
                c, h = vm[i, 4:28, :], vh[i, 4:28, :]
                zm, zh = shifted(c, h)
                s = vm[i - 1, 4:28, :] + vm[i + 1, 4:28, :] + vm[i, 3:27, :] + vm[i, 5:29, :] + zm
                t = vh[i - 1, 4:28, :] + vh[i + 1, 4:28, :] + vh[i, 3:27, :] + vh[i, 5:29, :] + zh
                new = jnp.where(mm[sel] > 0.5, (fm[i, 4:28, :] + s) * INV, c)
                newh = jnp.where(mh[sel] > 0.5, (fh[i, 4:28, :] + t) * INV, h)
                done.append((new, newh))
            for u in range(2):
                if last:
                    vm[x + u, 8:24, :] = done[u][0]
                else:
                    vm[x + u, 4:28, :] = done[u][0]
                    vh[x + u, 4:28, :] = done[u][1]

        planes0(lo, hi, body)

    arrive(ef0)
    unpack0(fm, fh, fx_r, fy_r, fxy_r, fz_r)

    def first0(x):
        for u in range(2):
            i = x + u
            sel = pick(base0, i, NGX * BX, 0)
            vm[i, 4:28, :] = jnp.where(mm[sel] > 0.5, fm[i, 4:28, :] * INV, 0.0)
            vh[i, 4:28, :] = jnp.where(mh[sel] > 0.5, fh[i, 4:28, :] * INV, 0.0)

    planes0(0, 40, first0)
    half0(1, 39, 1)
    half0(2, 38, 0)
    half0(3, 37, 1)

    def resid0(x):
        total = None
        for u in range(2):
            i = x + u
            c, h = vm[i, 8:24, :], vh[i, 8:24, :]
            zm, _ = shifted(c, h)
            s = vm[i - 1, 8:24, :] + vm[i + 1, 8:24, :] + vm[i, 7:23, :] + vm[i, 9:25, :] + zm
            r = fm[i, 8:24, :] - ((4.0 + 2.0 * BETA1) * c - s)
            total = r if total is None else total + r
        s0[(x - 4) // 2] = total

    planes0(4, 36, resid0)

    kk, cc = iota((128, 128), 0), iota((128, 128), 1)
    r01 = jnp.where((kk // 2 == cc - 6) & (cc >= 6) & (cc < 70), 0.5, 0.0)
    rows = []
    for x in range(16):
        rows.append(s0[x, pl.ds(0, 8, stride=2), :] + s0[x, pl.ds(1, 8, stride=2), :])
    b1 = jnp.dot(jnp.concatenate(rows, axis=0), r01, precision=HIGHEST, preferred_element_type=F32)
    for x in range(16):
        g1[6 + x, 16:24, :] = b1[8 * x : 8 * x + 8]

    def pack1(src, pk, zp):
        lo = jnp.zeros((8, 128), F32)
        hi = jnp.zeros((8, 128), F32)
        for t in range(8):
            a, b = src[6 + 2 * t, 16:24, :], src[7 + 2 * t, 16:24, :]
            pk[t] = jnp.where(lane < 64, roll(a, -6, 1), roll(b, 58, 1))
            for x, p in ((2 * t, a), (2 * t + 1, b)):
                lo = jnp.where(lane // 6 == x, roll(p, 6 * x - 6, 1), lo)
                hi = jnp.where(lane // 6 == x, roll(p, 6 * x - 64, 1), hi)
        zp[0] = lo
        zp[1] = hi

    def copies1(pk, zp, xr, yr, xyr, zr, ss, rs):
        out = []
        for k, d in enumerate(D26):
            dx, dy, dz = d
            if dz == 0 and dx == 0:
                s, t = pk, yr.at[side(-dy)]
            elif dz == 0:
                s = pk.at[pl.ds(0 if dx < 0 else 5, 3)]
                t = xr.at[side(-dx)] if dy == 0 else xyr.at[XY4.index((-dx, -dy))]
            else:
                s, t = zp.at[side(dz)], zr.at[Z18.index(neg(d))]
            out.append((d, pltpu.make_async_remote_copy(s, t, ss.at[k], rs.at[k], at(d), MESH)))
        return out

    def unpack1(dst, xr, yr, xyr, zr):
        for xe in range(28):
            nx, x = (-1, 10 + xe) if xe < 6 else ((0, xe - 6) if xe < 22 else (1, xe - 22))
            for ny in (-1, 0, 1):
                rows = slice(16 + 8 * ny, 24 + 8 * ny)
                if nx == 0 and ny == 0:
                    mid = dst[xe, rows, :]
                else:
                    if nx == 0:
                        mid = yr[side(ny), x // 2]
                    else:
                        tile = x // 2 - 5 if nx < 0 else x // 2
                        mid = xr[side(nx), tile] if ny == 0 else xyr[XY4.index((nx, ny)), tile]
                    mid = roll(mid, 6 if x % 2 == 0 else -58, 1)
                low = roll(zr[Z18.index((nx, ny, -1))], -6 * x, 1)
                high = roll(zr[Z18.index((nx, ny, 1))], 70 - 6 * x, 1)
                dst[xe, rows, :] = jnp.where(lane < 6, low, jnp.where(lane < 70, mid, high))

    ef1 = copies1(fk1, fz1, f1x_r, f1y_r, f1xy_r, f1z_r, s_f1, r_f1)
    ev1 = copies1(vk1, vz1, v1x_r, v1y_r, v1xy_r, v1z_r, s_v1, r_v1)
    pack1(g1, fk1, fz1)
    start(ef1)

    def half(v, g, m, base, total, lo, hi, colour):
        def run(j, carry):
            x = lo + 2 * j
            done = []
            for u in range(2):
                i = x + u
                sel = pick(base, i, total, colour)
                c = v[i, 8:32, :]
                s = v[i - 1, 8:32, :] + v[i + 1, 8:32, :] + v[i, 7:31, :] + v[i, 9:33, :]
                s = s + BETA1 * (roll(c, 1, 1) + roll(c, -1, 1))
                done.append(jnp.where(m[sel] > 0.5, (g[i, 8:32, :] + s) * INV, c))
            for u in range(2):
                v[x + u, 8:32, :] = done[u]
            return carry

        lax.fori_loop(0, (hi - lo) // 2, run, 0)

    def first(v, g, m, base, total, lo, hi):
        def run(j, carry):
            for u in range(2):
                i = lo + 2 * j + u
                sel = pick(base, i, total, 0)
                v[i, 8:32, :] = jnp.where(m[sel] > 0.5, g[i, 8:32, :] * INV, 0.0)
            return carry

        lax.fori_loop(0, (hi - lo) // 2, run, 0)

    def residual(v, g, i):
        c = v[i, 16:24, :]
        s = v[i - 1, 16:24, :] + v[i + 1, 16:24, :] + v[i, 15:23, :] + v[i, 17:25, :]
        s = s + BETA1 * (roll(c, 1, 1) + roll(c, -1, 1))
        return g[i, 16:24, :] - ((4.0 + 2.0 * BETA1) * c - s)

    arrive(ef1)
    unpack1(g1, f1x_r, f1y_r, f1xy_r, f1z_r)
    lev1 = (v1, g1, m1, base1, NGX * 16)
    first(*lev1, 2, 26)
    half(*lev1, 3, 25, 1)
    half(*lev1, 4, 24, 0)
    half(*lev1, 5, 23, 1)
    for x in range(8):
        s1[8 * x : 8 * x + 8, :] = residual(v1, g1, 6 + 2 * x) + residual(v1, g1, 7 + 2 * x)

    r12 = jnp.where(((kk - 6) // 2 == cc - 7) & (kk >= 6) & (kk < 70) & (cc >= 7) & (cc < 39), 0.5, 0.0)
    rows = []
    for y in range(4):
        rows.append(s1[pl.ds(2 * y, 8, stride=8), :] + s1[pl.ds(2 * y + 1, 8, stride=8), :])
    b2 = jnp.dot(jnp.concatenate(rows, axis=0), r12, precision=HIGHEST, preferred_element_type=F32)
    for y in range(4):
        g2[7 + y, 16:24, :] = b2[8 * y : 8 * y + 8]

    def pack2(src, t):
        acc = jnp.zeros((8, 128), F32)
        for y in range(4):
            acc = jnp.where(lane // 32 == y, roll(src[7 + y, 16:24, :], 32 * y - 7, 1), acc)
        t[...] = acc

    def copies2(t, tr, ss, rs):
        out = []
        for k, d in enumerate(D44):
            out.append(
                (d, pltpu.make_async_remote_copy(t, tr.at[D44.index(neg(d))], ss.at[k], rs.at[k], at(d), MESH))
            )
        return out

    def unpack2(dst, own, tr, which):
        for ny in which:
            if ny == -2:
                ys = [(i, 1 + i) for i in range(3)]
            elif ny == 2:
                ys = [(15 + i, i) for i in range(3)]
            else:
                ys = [(7 + 4 * ny + i, i) for i in range(4)]
            for nx in (-1, 0, 1):
                rows = slice(16 + 8 * nx, 24 + 8 * nx)
                mid = own[...] if (nx, ny) == (0, 0) else tr[D44.index((nx, ny, 0))]
                low, high = tr[D44.index((nx, ny, -1))], tr[D44.index((nx, ny, 1))]
                for e, y in ys:
                    a = roll(low, -25 - 32 * y, 1)
                    b = roll(mid, 7 - 32 * y, 1)
                    c = roll(high, 39 - 32 * y, 1)
                    dst[e, rows, :] = jnp.where(lane < 7, a, jnp.where(lane < 39, b, c))

    ef2 = copies2(ft2, f2_r, s_f2, r_f2)
    ev2 = copies2(vt2, v2_r, s_v2, r_v2)
    pack2(g2, ft2)
    start(ef2)
    arrive([(d, c) for d, c in ef2 if abs(d[1]) < 2])
    unpack2(g2, ft2, f2_r, (-1, 0, 1))
    lev2 = (v2, g2, m2, base2, NGY * 4)
    first(*lev2, 3, 15)
    half(*lev2, 4, 14, 1)
    half(*lev2, 5, 13, 0)
    half(*lev2, 6, 12, 1)
    for y in range(2):
        s2[8 * y : 8 * y + 8, :] = residual(v2, g2, 7 + 2 * y) + residual(v2, g2, 8 + 2 * y)

    r23 = jnp.where(((kk - 7) // 2 == cc % 16) & (kk >= 7) & (kk < 39), 0.5, 0.0)
    a3 = s2[pl.ds(0, 8, stride=2), :] + s2[pl.ds(1, 8, stride=2), :]
    b3 = jnp.dot(a3, r23, precision=HIGHEST, preferred_element_type=F32)
    b3 = jnp.sum(jnp.where(lane // 16 == row, b3, 0.0), axis=0, keepdims=True)
    t3[...] = jnp.where(row == iy, b3, 0.0)

    egy, egz, egx = [], [], []
    for k in range(1, NGY):
        peer = (ix, lax.rem(iy + k, NGY), iz)
        egy.append(pltpu.make_async_remote_copy(t3, gy_r.at[k - 1], s_g.at[k - 1], r_g.at[k - 1], peer, MESH))
    for k in range(1, NGZ):
        peer = (ix, iy, lax.rem(iz + k, NGZ))
        n = 6 + k
        egz.append(pltpu.make_async_remote_copy(gzb.at[iz], gzb.at[iz], s_g.at[n], r_g.at[n], peer, MESH))
    for k in range(1, NGX):
        peer = (lax.rem(ix + k, NGX), iy, iz)
        n = 9 + k
        egx.append(pltpu.make_async_remote_copy(gzb, gxb.at[ix], s_g.at[n], r_g.at[n], peer, MESH))

    for c in egy:
        c.start()
    pack2(v2, vt2)
    pack1(v1, vk1, vz1)
    pack0(vm, vy0, vz0)
    arrive([(d, c) for d, c in ef2 if abs(d[1]) == 2])
    unpack2(g2, ft2, f2_r, (-2, 2))
    for c in egy:
        c.wait_recv()
    line = t3[...]
    for k in range(NGY - 1):
        line = line + gy_r[k]
    gzb[iz] = line
    for c in egz:
        c.start()
    for c in egz:
        c.wait_recv()
    for c in egx:
        c.start()
    start(ev2)
    start(ev1)
    start(ev0)
    gxb[ix] = gzb[...]
    for c in egx:
        c.wait_recv()

    for gx in range(NGX):
        for xl in range(4):
            acc = jnp.zeros((8, 128), F32)
            for gz in range(NGZ):
                acc = jnp.where((lane % 64) // 16 == gz, roll(gxb[gx, gz], (gz - xl) * 16, 1), acc)
            g3[4 * gx + xl] = acc

    zl = lane % 64
    w_lo = jnp.where(zl == 0, 0.0, BETA1)
    w_hi = jnp.where(zl == 63, 0.0, BETA1)
    y_edge = jnp.where(((row == 0) & (lane < 64)) | ((row == 7) & (lane >= 64)), 0.0, 1.0)
    par3 = (lane // 64 + lane) & 1
    colours3 = (par3 == 0, par3 == 1)

    def sum3(x):
        c = v3[x + 4]
        a = roll(c, 64, 1)
        w = jnp.where(lane < 64, roll(a, 1, 0), roll(a, -1, 0)) * y_edge
        s = v3[x + 3] + v3[x + 5] + (a + w)
        return c, s + (roll(c, 1, 1) * w_lo + roll(c, -1, 1) * w_hi)

    def half3(colour):
        def run(j, carry):
            done = []
            for u in range(4):
                x = 4 * j + u
                c, s = sum3(x)
                done.append(jnp.where(colours3[(u + colour) % 2], (g3[x] + s) * INV, c))
            for u in range(4):
                v3[4 * j + u + 4] = done[u]
            return carry

        lax.fori_loop(0, 8, run, 0)

    def first3(j, carry):
        for u in range(2):
            v3[2 * j + u + 4] = jnp.where(colours3[u], g3[2 * j + u] * INV, 0.0)
        return carry

    lax.fori_loop(0, 16, first3, 0)
    half3(1)
    half3(0)
    half3(1)

    def small(g, level):
        n = len(g)
        dz, dy = 2 ** (level - 3), 2 ** (level - 4)
        lo = jnp.where(zl < dz, 0.0, BETA1)
        hi = jnp.where(zl >= 64 - dz, 0.0, BETA1)
        ylo = jnp.where(row < dy, 0.0, 1.0)
        yhi = jnp.where(row >= 8 - dy, 0.0, 1.0)
        par = (row // dy + zl // dz) & 1
        colours = (par == 0, par == 1)

        def total(v, x):
            c = v[x]
            s = roll(c, dz, 1) * lo + roll(c, -dz, 1) * hi
            s = s + (roll(c, dy, 0) * ylo + roll(c, -dy, 0) * yhi)
            if x > 0:
                s = s + v[x - 1]
            if x < n - 1:
                s = s + v[x + 1]
            return s

        def sweep(v, colour):
            return [
                jnp.where(colours[(x + colour) % 2], (g[x] + total(v, x)) * INV, v[x]) for x in range(n)
            ]

        def black_from_red(v):
            return sweep(v, 1)

        v = [jnp.where(colours[x % 2], g[x] * INV, 0.0) for x in range(n)]
        v = sweep(v, 1)
        if level == 6:
            for _ in range(CSWEEPS - 1):
                v = sweep(sweep(v, 0), 1)
            return v
        v = sweep(sweep(v, 0), 1)
        r = [g[x] - ((4.0 + 2.0 * BETA1) * v[x] - total(v, x)) for x in range(n)]
        coarse = []
        for x in range(n // 2):
            t = r[2 * x] + r[2 * x + 1]
            t = t + jnp.where((row // dy) % 2 == 0, roll(t, -dy, 0), roll(t, dy, 0))
            t = t + jnp.where((zl // dz) % 2 == 0, roll(t, -dz, 1), roll(t, dz, 1))
            coarse.append(0.5 * t)
        e = small(coarse, level + 1)
        v = [v[x] + e[x // 2] for x in range(n)]
        for _ in range(2):
            v = sweep(sweep(v, 0), 1)
        return v

    def resid3(x):
        c, s = sum3(x)
        return g3[x] - ((4.0 + 2.0 * BETA1) * c - s)

    g4 = []
    for x in range(16):
        t = resid3(2 * x) + resid3(2 * x + 1)
        t = t + roll(t, 64, 1)
        t = t + jnp.where(lane % 2 == 0, roll(t, -1, 1), roll(t, 1, 1))
        g4.append(0.5 * t)
    e4 = small(g4, 4)
    for x in range(32):
        v3[4 + x] = v3[4 + x] + e4[x // 2]
    for _ in range(2):
        half3(0)
        half3(1)

    k2, c2 = iota((128, 256), 0), iota((128, 256), 1)
    cl = c2 % 128
    zc = iz * 16 + (cl + 1) // 2 - 4
    p32 = jnp.where((zc >= 0) & (zc < 64) & (cl < 46) & (k2 == (c2 // 128) * 64 + zc), 1.0, 0.0)
    e3 = v3[pl.ds(4 * ix, 12)].reshape(96, 128)
    u3 = jnp.dot(e3, p32, precision=HIGHEST, preferred_element_type=F32)
    for yl in range(2):
        tmp2[yl, 16:112, :] = u3[:, 128 * yl : 128 * yl + 128]
    for j in range(10):
        first_row = 16 + iy - 2 + j // 2
        e = tmp2[j % 2, pl.ds(first_row, 12, stride=8), :]
        pe2[j, pl.ds(0, 12, stride=2), :] = e
        pe2[j, pl.ds(1, 12, stride=2), :] = e
    arrive(ev2)
    unpack2(v2, vt2, v2_r, (-2, -1, 0, 1, 2))
    for i in range(18):
        sel = picked(base2, i, NGY * 4)
        v2[i, 8:32, :] = jnp.where(m2[sel] > 0.5, v2[i, 8:32, :] + pe2[(i + 1) // 2], 0.0)
    half(*lev2, 1, 17, 0)
    half(*lev2, 2, 16, 1)
    half(*lev2, 3, 15, 0)
    half(*lev2, 4, 14, 1)

    p21 = jnp.where((cc < 76) & (kk == 4 + cc // 2), 1.0, 0.0)
    u2 = jnp.dot(v2[3:15, 8:32, :].reshape(288, 128), p21, precision=HIGHEST, preferred_element_type=F32)
    tmp1[...] = u2
    for k in range(14):
        e = tmp1[pl.ds(5 + k, 12, stride=24), :]
        pe1[k, pl.ds(0, 12, stride=2), :] = e
        pe1[k, pl.ds(1, 12, stride=2), :] = e
    arrive(ev1)
    unpack1(v1, v1x_r, v1y_r, v1xy_r, v1z_r)
    for i in range(28):
        sel = picked(base1, i, NGX * 16)
        v1[i, 8:32, :] = jnp.where(m1[sel] > 0.5, v1[i, 8:32, :] + pe1[i // 2], 0.0)
    half(*lev1, 1, 27, 0)
    half(*lev1, 2, 26, 1)
    half(*lev1, 3, 25, 0)
    half(*lev1, 4, 24, 1)

    main_lane = 6 + cl // 2
    halo_lane = jnp.where(cl < 64, 70 + cl // 2, 6 + (cl - 128) // 2)
    used = (c2 < 128) | (cl < 4) | (cl >= 124)
    p10 = jnp.where(used & (k2 == jnp.where(c2 < 128, main_lane, halo_lane)), 1.0, 0.0)
    u1 = jnp.dot(v1[4:24, 14:30, :].reshape(320, 128), p10, precision=HIGHEST, preferred_element_type=F32)
    tmp0[...] = u1
    for k in range(20):
        for ref, cols in ((pe0m, slice(0, 128)), (pe0h, slice(128, 256))):
            e = tmp0[16 * k : 16 * k + 12, cols]
            ref[k, pl.ds(0, 12, stride=2), :] = e
            ref[k, pl.ds(1, 12, stride=2), :] = e
    arrive(ev0)
    sent(ev0)
    unpack0(vm, vh, vx_r, vy_r, vxy_r, vz_r)

    def add0(x):
        for u in range(2):
            i = x + u
            k = x // 2
            sel = picked(base0, i, NGX * BX)
            vm[i, 4:28, :] = jnp.where(mm[sel] > 0.5, vm[i, 4:28, :] + pe0m[k], 0.0)
            vh[i, 4:28, :] = jnp.where(mh[sel] > 0.5, vh[i, 4:28, :] + pe0h[k], 0.0)

    planes0(0, 40, add0)
    half0(1, 39, 0)
    half0(2, 38, 1)
    half0(3, 37, 0)
    half0(4, 36, 1, last=True)

    store = pltpu.make_async_copy(vm.at[pl.ds(4, BX), pl.ds(8, BY), :], out_hbm, io_sem.at[1])
    store.start()
    for e in (ef0, ef1, ef2, ev2, ev1):
        sent(e)
    for c in egy + egz + egx:
        c.wait_send()
    store.wait()


def on_device(density):
    def vmem(*shape):
        return pltpu.VMEM(shape, F32)

    level0 = [vmem(40, 32, 128)] * 4 + [vmem(4, 24, 128)] * 2
    level0 += [vmem(16, 16, 128), vmem(20, 24, 128), vmem(20, 24, 128), vmem(320, 256)]
    level1 = [vmem(28, 40, 128)] * 2 + [vmem(4, 24, 128), vmem(64, 128), vmem(14, 24, 128), vmem(288, 128)]
    level2 = [vmem(18, 40, 128)] * 2 + [vmem(4, 24, 128), vmem(16, 128), vmem(10, 24, 128), vmem(2, 128, 128)]
    packs = [vmem(2, 16, 8, 128), vmem(2, 16, 128)] * 2 + [vmem(8, 8, 128), vmem(2, 8, 128)] * 2
    packs += [vmem(8, 128)] * 2
    recv0 = [vmem(2, 4, 16, 128), vmem(2, 16, 8, 128), vmem(4, 2, 8, 128), vmem(18, 16, 128)] * 2
    recv1 = [vmem(2, 3, 8, 128), vmem(2, 8, 8, 128), vmem(4, 3, 8, 128), vmem(18, 8, 128)] * 2
    recv2 = [vmem(44, 8, 128)] * 2
    gather = [vmem(8, 128), vmem(7, 8, 128), vmem(4, 8, 128), vmem(8, 4, 8, 128), vmem(32, 8, 128), vmem(40, 8, 128)]
    dma = pltpu.SemaphoreType.DMA
    sems = [dma((2,))] + [dma((26,))] * 8 + [dma((44,))] * 4 + [dma((17,))] * 2
    return pl.pallas_call(
        kernel,
        out_shape=jax.ShapeDtypeStruct((BX, BY, BZ), F32),
        in_specs=[pl.BlockSpec(memory_space=pl.ANY)],
        out_specs=pl.BlockSpec(memory_space=pl.ANY),
        scratch_shapes=level0 + level1 + level2 + packs + recv0 + recv1 + recv2 + gather + sems,
        compiler_params=pltpu.CompilerParams(
            collective_id=0, has_side_effects=True, vmem_limit_bytes=48 * 1024 * 1024
        ),
    )(density)


def solution(mesh):
    spec = P("gx", "gy", "gz")
    return jax.shard_map(on_device, mesh=mesh, in_specs=(spec,), out_specs=spec, check_vma=False)
```

time: 524 us -> 80.3 us (0.15)
  starting transfers between devices: 221 us -> 0 us
  waiting for transfers between devices: 170 us -> 0 us
  Pallas kernels: 0 us -> 78.5 us
  blocking collectives: 51.8 us -> 0 us
  local copies, waits for them, and re-layouts: 39.1 us -> 1.65 us
  other arithmetic: 36.1 us -> 0 us
    ppermute x90 -> x0, starting transfers between devices: 221 us -> none  [the longest x36 115 us: extended_2(): before = lax.ppermute(last, axis, up)]
    ppermute x90 -> x0, waiting for transfers between devices: 170 us -> none  [the longest x36 125 us: extended_2(): after = lax.ppermute(leading, axis, down)]
    pallas_call x0 -> x1, Pallas kernels: none -> 78.5 us  [on_device(): pl.pallas_call(kernel, out_shape=jax.ShapeDtypeStruct((BX, BY, BZ), F32),...]
    all_gather x4 -> x0, blocking collectives: 51.8 us -> none  [stacked_from(): pieces = lax.all_gather(pieces, axes[k])]
    reshape x19 -> x0, local copies, waits for them, and re-layouts: 33.4 us -> none  [the longest x6 31.1 us: restrict(): residue.reshape(shape[0] // 2, 2, shape[1] // 2, 2, shape[2] // 2, 2)]
    select_n x55 -> x0, other arithmetic: 19.2 us -> none  [the longest x12 9.74 us: wide_sweep(): extended = jnp.where(red_wide, update, extended)]
    reduce_sum x6 -> x0, other arithmetic: 11.7 us -> none  [restrict(): return jnp.mean(blocks, axis=(1, 3, 5))]
  transfers between devices with their start and end apart: 90 -> 0, of which waited for: 50 -> 0; matrix products, arithmetic and copies ran while one was open for 0% -> 0% of each run, Pallas kernels for 0% -> 0%
where the time goes in v1:
time: 80.3 us; the launch traced here: 80.2 us
  Pallas kernels  78.5 us (98%)
  local copies, waits for them, and re-layouts  1.65 us (2%)
    pallas_call x1, Pallas kernels, on_device(): pl.pallas_call(kernel, out_shape=jax.ShapeDtypeStruct((BX, BY, BZ), F32),...  78.5 us
    unnamed x3, local copies, waits for them, and re-layouts  1.65 us

profile of v1, /device:TPU:1, one launch (start us, length us, event | category | flops | bytes accessed | tf_op | source)
XLA Modules:
  0.0 80.2 jit_solution(7114382156343367616)
XLA Ops:
  0.0 0.0 copy-start
  0.0 0.9 %copy-done = f32[32,16,128]{2,1,0:T(8,128)S(1)} copy-done((f32[32,16,128]{2,1,0:T(8,128)S(1)}, f32[32,16,128]{2,1,0:T(8,128)}, u32[]{:S(2)}) %copy-start) | copy-done | bytes 262168
  1.0 78.5 %shard_map.17 = f32[32,16,128]{2,1,0:T(8,128)S(1)} custom-call(f32[32,16,128]{2,1,0:T(8,128)S(1)} %copy-done), custom_call_target="tpu_custom_call" | custom-call | tf_op jit(solution)/shard_map/pallas_call | solution.py:716
  79.5 0.7 copy.3
Async XLA Ops:
  0.0 0.9 %copy-start = (f32[32,16,128]{2,1,0:T(8,128)S(1)}, f32[32,16,128]{2,1,0:T(8,128)}, u32[]{:S(2)}) copy-start(f32[32,16,128]{2,1,0:T(8,128)} %f_hbm.1) | copy-start | bytes 786436

commit v2 on v1

v2 whole, which is shorter than its diff:
```python
import itertools

import jax
import jax.numpy as jnp
from jax import lax
from jax.experimental import pallas as pl
from jax.experimental.pallas import tpu as pltpu
from jax.sharding import PartitionSpec as P

MESH = pl.DeviceIdType.MESH
F32 = jnp.float32
BF16 = jnp.bfloat16

NGX, NGY, NGZ = 8, 8, 4
BX, BY, BZ = 32, 16, 128
CSWEEPS = 4
BETA1 = 1.5
CENTRE = 4.0 + 2.0 * BETA1
INV = 1.0 / CENTRE

D26 = [d for d in itertools.product((-1, 0, 1), repeat=3) if d != (0, 0, 0)]
D44 = [d for d in itertools.product((-1, 0, 1), (-2, -1, 0, 1, 2), (-1, 0, 1)) if d != (0, 0, 0)]
XY4 = [(-1, -1), (-1, 1), (1, -1), (1, 1)]
Z18 = [d for d in D26 if d[2] != 0]


def roll(x, shift, axis):
    size = x.shape[axis]
    shift = shift % size
    return x if shift == 0 else pltpu.roll(x, shift, axis)


def iota(shape, dim):
    return lax.broadcasted_iota(jnp.int32, shape, dim)


def side(n):
    return 0 if n < 0 else 1


def neg(n):
    return (-n[0], -n[1], -n[2])


def moved(x, matrix):
    hi = x.astype(BF16)
    rest = x - hi.astype(F32)
    mid = rest.astype(BF16)
    lo = (rest - mid.astype(F32)).astype(BF16)
    return (
        jnp.dot(lo, matrix, preferred_element_type=F32)
        + jnp.dot(mid, matrix, preferred_element_type=F32)
        + jnp.dot(hi, matrix, preferred_element_type=F32)
    )


def kernel(
    f_hbm, out_hbm,
    f0, p0, fr0, fb0, vr0, vb0, k0, s0, pe0, out,
    fr1, fb1, vr1, vb1, k1, s1, pe1, tmp1,
    fr2, fb2, vr2, vb2, k2, s2, pe2, tmp2,
    fy0, fz0, vy0, vz0, fk1, fz1, vk1, vz1, ft2, vt2,
    fx_r, fy_r, fxy_r, fz_r, vx_r, vy_r, vxy_r, vz_r,
    f1x_r, f1y_r, f1xy_r, f1z_r, v1x_r, v1y_r, v1xy_r, v1z_r,
    f2_r, v2_r,
    t3, gy_r, gzb, gxb, g3, v3,
    io_sem, s_f0, r_f0, s_v0, r_v0, s_f1, r_f1, s_v1, r_v1, s_f2, r_f2, s_v2, r_v2, s_g, r_g,
):
    ix, iy, iz = lax.axis_index("gx"), lax.axis_index("gy"), lax.axis_index("gz")

    def there(n):
        nx, ny, nz = ix + n[0], iy + n[1], iz + n[2]
        return (nx >= 0) & (nx < NGX) & (ny >= 0) & (ny < NGY) & (nz >= 0) & (nz < NGZ)

    def at(n):
        return (
            jnp.clip(ix + n[0], 0, NGX - 1),
            jnp.clip(iy + n[1], 0, NGY - 1),
            jnp.clip(iz + n[2], 0, NGZ - 1),
        )

    load = pltpu.make_async_copy(f_hbm, f0, io_sem.at[0])
    load.start()

    barrier = pltpu.get_barrier_semaphore()
    count = 0
    for d in D44:
        ok = there(d)
        count = count + ok.astype(jnp.int32)

        @pl.when(ok)
        def _(d=d):
            pl.semaphore_signal(barrier, inc=1, device_id=at(d), device_id_type=MESH)

    lines = []
    for k in range(1, NGY):
        lines.append((ix, lax.rem(iy + k, NGY), iz))
    for k in range(1, NGZ):
        lines.append((ix, iy, lax.rem(iz + k, NGZ)))
    for k in range(1, NGX):
        lines.append((lax.rem(ix + k, NGX), iy, iz))
    for peer in lines:
        pl.semaphore_signal(barrier, inc=1, device_id=peer, device_id_type=MESH)

    lane = iota((8, 128), 1)
    row = iota((8, 128), 0)
    lane16 = iota((16, 128), 1)
    r32, l32 = iota((32, 128), 0), iota((32, 128), 1)
    signed = jnp.where(l32 < 96, l32, l32 - 128)

    def fill(ref, halo, pairs, start_pairs, total_pairs, rows_at, total_rows):
        zp = start_pairs + signed
        ok = (signed >= -halo) & (signed < pairs + halo) & (zp >= 0) & (zp < total_pairs)
        ok = ok & (rows_at >= 0) & (rows_at < total_rows)
        ref[0] = jnp.zeros((32, 128), F32)
        ref[1] = jnp.where(ok, INV, 0.0)

    fill(k0, 2, 64, iz * 64, NGZ * 64, iy * BY + r32 - 8, NGY * BY)
    fill(k1, 3, 32, iz * 32, NGZ * 32, iy * 8 + r32 - 16, NGY * 8)
    fill(k2, 4, 16, iz * 16, NGZ * 16, ix * 8 + r32 - 16, NGX * 8)

    class Level:
        def __init__(self, fr, fb, vr, vb, k, first, main, rows, window, odd, start, total):
            self.fr, self.fb, self.vr, self.vb, self.k = fr, fb, vr, vb, k
            self.first, self.main, self.rows, self.window = first, main, rows, window
            self.odd, self.start, self.total = odd, start, total
            self.planes = main + 2 * first

        def coefficient(self, i, lo, hi):
            if self.first <= i < self.first + self.main:
                return self.k[1, lo:hi, :]
            pos = self.start + i
            return self.k[jnp.where((pos >= 0) & (pos < self.total), 1, 0), lo:hi, :]

        def even(self, i, lo, hi):
            return (iota((hi - lo, 128), 0) + (lo + i + self.odd)) % 2 == 0

    lev0 = Level(fr0, fb0, vr0, vb0, k0, 4, BX, (8, 24), (4, 28), 0, ix * BX - 4, NGX * BX)
    lev1 = Level(fr1, fb1, vr1, vb1, k1, 6, 16, (16, 24), (8, 32), 0, ix * 16 - 6, NGX * 16)
    lev2 = Level(fr2, fb2, vr2, vb2, k2, 7, 4, (16, 24), (8, 32), 1, iy * 4 - 7, NGY * 4)

    def around(level, src, i, lo, hi, red):
        c = src[i, lo:hi, :]
        up, down = roll(c, 1, 1), roll(c, -1, 1)
        even = level.even(i, lo, hi)
        z = jnp.where(even, up, down) if red else jnp.where(even, down, up)
        s = (src[i - 1, lo:hi, :] + src[i + 1, lo:hi, :]) + (
            src[i, lo - 1 : hi - 1, :] + src[i, lo + 1 : hi + 1, :]
        )
        return s + BETA1 * (c + z)

    def half(level, lo, hi, red, rows=None):
        dst, src = (level.vr, level.vb) if red else (level.vb, level.vr)
        source = level.fr if red else level.fb
        a, b = rows or level.window
        for i in range(lo, hi):
            s = source[i, a:b, :] + around(level, src, i, a, b, red)
            dst[i, a:b, :] = s * level.coefficient(i, a, b)

    def first_half(level, lo, hi):
        a, b = level.window
        for i in range(lo, hi):
            level.vr[i, a:b, :] = level.fr[i, a:b, :] * level.coefficient(i, a, b)

    def smooth_down(level):
        n, m = level.first, level.first + level.main
        first_half(level, n - 4, m + 4)
        half(level, n - 3, m + 3, False)
        half(level, n - 2, m + 2, True)
        half(level, n - 1, m + 1, False)

    def residual(level, i):
        a, b = level.rows
        vr, vb = level.vr[i, a:b, :], level.vb[i, a:b, :]
        red = level.fr[i, a:b, :] - (CENTRE * vr - around(level, level.vb, i, a, b, True))
        black = level.fb[i, a:b, :] - (CENTRE * vb - around(level, level.vr, i, a, b, False))
        return red + black

    def zero(ref):
        @pl.loop(0, ref.shape[0])
        def _(i):
            ref[i] = jnp.zeros(ref.shape[1:], F32)

    for ref in (vr0, vb0, vr1, vb1, vr2, vb2, pe0, pe1, pe2, v3, tmp2):
        zero(ref)

    def splitter(total, where):
        k, c = iota((256, total), 0), iota((256, total), 1)
        z = k % 128
        return z, (z + k // 128) % 2 == 0, c, where

    def split_rows(a, even):
        return jnp.concatenate([jnp.where(even, a, 0.0), jnp.where(even, 0.0, a)], axis=1)

    k256, c128 = iota((256, 128), 0), iota((256, 128), 1)
    z256 = k256 % 128
    red256 = (z256 + k256 // 128) % 2 == 0

    load.wait()

    to_pairs = jnp.where(c128 == z256 // 2 + jnp.where(red256, 0, 64), 1.0, 0.0).astype(BF16)
    for part in range(4):
        rows = []
        for x in range(8 * part, 8 * part + 8):
            rows.append(split_rows(f0[x], (iota((16, 128), 0) + x) % 2 == 0))
        p = moved(jnp.concatenate(rows, axis=0), to_pairs)
        for x in range(8):
            p0[8 * part + x] = p[16 * x : 16 * x + 16]

    def pack0(plane, yp, zp):
        lo = jnp.zeros((16, 128), F32)
        hi = jnp.zeros((16, 128), F32)
        slot = (lane16 % 64) // 2
        for x in range(BX):
            p = plane(x)
            half_tile = slice(4 * (x % 2), 4 * (x % 2) + 4)
            yp[0, x // 2, half_tile, :] = p[0:4]
            yp[1, x // 2, half_tile, :] = p[12:16]
            t = roll(p, 2 * x, 1)
            lo = jnp.where(slot == x, t, lo)
            hi = jnp.where(slot == (x - 1) % BX, roll(p, 64, 1) if x == 0 else t, hi)
        zp[0] = lo
        zp[1] = hi

    def copies0(xs, yp, zp, xr, yr, xyr, zr, ss, rs):
        out = []
        for k, d in enumerate(D26):
            dx, dy, dz = d
            if dz == 0 and dy == 0:
                s, t = xs(dx), xr.at[side(-dx)]
            elif dz == 0 and dx == 0:
                s, t = yp.at[side(dy)], yr.at[side(-dy)]
            elif dz == 0:
                s = yp.at[side(dy), pl.ds(0 if dx < 0 else 14, 2)]
                t = xyr.at[XY4.index((-dx, -dy))]
            else:
                slot = Z18.index(neg(d))
                if dy == 0:
                    s, t = zp.at[side(dz)], zr.at[slot]
                else:
                    rows = pl.ds(0 if dy < 0 else 8, 8)
                    s, t = zp.at[side(dz), rows], zr.at[slot, rows]
            out.append((d, pltpu.make_async_remote_copy(s, t, ss.at[k], rs.at[k], at(d), MESH)))
        return out

    def start(copies):
        for d, c in copies:
            @pl.when(there(d))
            def _(c=c):
                c.start()

    def arrive(copies):
        for d, c in copies:
            @pl.when(there(neg(d)))
            def _(c=c):
                c.wait_recv()

    def sent(copies):
        for d, c in copies:
            @pl.when(there(d))
            def _(c=c):
                c.wait_send()

    def unpack0(own, xr, yr, xyr, zr, put, colours):
        for nx in (-1, 0, 1):
            for ny, src, dst, num in ((-1, 8, 0, 8), (0, 0, 8, 16), (1, 0, 24, 8)):
                low = zr[Z18.index((nx, ny, -1)), src : src + num, :]
                high = zr[Z18.index((nx, ny, 1)), src : src + num, :]
                lanes = iota((num, 128), 1)
                mixed = [jnp.where(lanes < 64, high, low), jnp.where(lanes < 64, low, high)]
                xs = range(28, 32) if nx < 0 else (range(32) if nx == 0 else range(4))
                for x in xs:
                    if ny == 0:
                        p = own(x) if nx == 0 else xr[side(nx), x % 4]
                    else:
                        if nx == 0:
                            p = yr[side(ny), x // 2]
                        else:
                            p = xyr[XY4.index((nx, ny)), (x % 4) // 2]
                        if (x % 2 == 0) == (ny < 0):
                            p = roll(p, 4, 0)
                    for colour in range(colours):
                        if x == 0:
                            a = roll(high, 64 if colour == 0 else 0, 1)
                            b = roll(low, 0 if colour == 0 else 64, 1)
                            e = jnp.where(lanes < 96, a, b)
                        else:
                            e = roll(mixed[colour], (64 if colour == 0 else 0) - 2 * x, 1)
                        q = p if colour == 0 else roll(p, 64, 1)
                        i = 32 * nx + x + 4
                        put(colour, i, dst, num, jnp.where(lanes < 64, q, e))

    def clean(level):
        def put(colour, i, dst, num, value):
            ok = level.coefficient(i, dst, dst + num) > 0.0
            (level.fr if colour == 0 else level.fb)[i, dst : dst + num, :] = jnp.where(ok, value, 0.0)

        return put

    def corrected(level, add):
        def put(colour, i, dst, num, value):
            ok = level.coefficient(i, dst, dst + num) > 0.0
            level.vb[i, dst : dst + num, :] = jnp.where(ok, value + add(i, dst, num), 0.0)

        return put

    ef0 = copies0(
        lambda dx: p0.at[pl.ds(0 if dx < 0 else 28, 4)], fy0, fz0, fx_r, fy_r, fxy_r, fz_r, s_f0, r_f0
    )
    ev0 = copies0(
        lambda dx: vb0.at[pl.ds(4 if dx < 0 else 32, 4), pl.ds(8, BY), :],
        vy0, vz0, vx_r, vy_r, vxy_r, vz_r, s_v0, r_v0,
    )

    pack0(lambda x: p0[x], fy0, fz0)
    pl.semaphore_wait(barrier, count + len(lines))
    start(ef0)

    split1 = iota((256, 256), 1)
    k1i = iota((256, 256), 0)
    z1i = k1i % 128
    red1 = (z1i + k1i // 128) % 2 == 0
    packed = (split1 < 128) & (split1 % 64 == z1i // 2 + jnp.where(red1, 0, 32))
    apart = (split1 >= 128) & (split1 - 128 == z1i // 2 + jnp.where(red1, 0, 64))
    to_pairs1 = jnp.where((z1i < 64) & (packed | apart), 0.5, 0.0).astype(BF16)
    to_pairs2 = jnp.where(
        (z256 < 32) & (c128 % 32 == z256 // 2 + jnp.where(red256, 0, 16)), 0.5, 0.0
    ).astype(BF16)
    csign = jnp.where(c128 < 96, c128, c128 - 128)
    wanted = ((csign + 128) // 2 - 64) % 128 + 128 * ((csign + 128) % 2)
    from_pairs = jnp.where((k256 == wanted) & (csign >= -4) & (csign < 68), 1.0, 0.0).astype(BF16)
    to_cells = jnp.where(k256 == c128 // 2 + 128 * (c128 % 2), 1.0, 0.0).astype(BF16)

    arrive(ef0)
    unpack0(lambda x: p0[x], fx_r, fy_r, fxy_r, fz_r, clean(lev0), 2)
    smooth_down(lev0)
    for x in range(16):
        s0[x] = residual(lev0, 4 + 2 * x) + residual(lev0, 5 + 2 * x)

    rows = []
    for x in range(16):
        a = s0[x, pl.ds(0, 8, stride=2), :] + s0[x, pl.ds(1, 8, stride=2), :]
        rows.append(split_rows(a, (row + x) % 2 == 0))
    b1 = moved(jnp.concatenate(rows, axis=0), to_pairs1)

    def zpack1(plane, zp):
        lo = jnp.zeros((8, 128), F32)
        hi = jnp.zeros((8, 128), F32)
        for x in range(16):
            p = plane(x)
            here = (lane % 64) // 3 == x
            lo = jnp.where(here, roll(p, 3 * x, 1), lo)
            hi = jnp.where(here, roll(p, 3 * x - 29, 1), hi)
        zp[0] = lo
        zp[1] = hi

    def copies1(pk, zp, xr, yr, xyr, zr, ss, rs):
        out = []
        for k, d in enumerate(D26):
            dx, dy, dz = d
            if dz == 0 and dx == 0:
                s, t = pk, yr.at[side(-dy)]
            elif dz == 0:
                s = pk.at[pl.ds(0 if dx < 0 else 5, 3)]
                t = xr.at[side(-dx)] if dy == 0 else xyr.at[XY4.index((-dx, -dy))]
            else:
                s, t = zp.at[side(dz)], zr.at[Z18.index(neg(d))]
            out.append((d, pltpu.make_async_remote_copy(s, t, ss.at[k], rs.at[k], at(d), MESH)))
        return out

    def unpack1(pk, xr, yr, xyr, zr, put, colours):
        for xe in range(28):
            nx, x = (-1, 10 + xe) if xe < 6 else ((0, xe - 6) if xe < 22 else (1, xe - 22))
            for ny in (-1, 0, 1):
                if nx == 0:
                    mid = pk[x // 2] if ny == 0 else yr[side(ny), x // 2]
                else:
                    tile = x // 2 - 5 if nx < 0 else x // 2
                    mid = xr[side(nx), tile] if ny == 0 else xyr[XY4.index((nx, ny)), tile]
                low, high = zr[Z18.index((nx, ny, -1))], zr[Z18.index((nx, ny, 1))]
                for colour in range(colours):
                    a = roll(mid, -64 * (x % 2) - 32 * colour, 1)
                    b = roll(high, 32 - 3 * x - 64 * colour, 1)
                    c = roll(low, 125 - 3 * x - 64 * colour, 1)
                    put(colour, xe, 16 + 8 * ny, 8, jnp.where(lane < 32, a, jnp.where(lane < 64, b, c)))

    ef1 = copies1(fk1, fz1, f1x_r, f1y_r, f1xy_r, f1z_r, s_f1, r_f1)
    ev1 = copies1(vk1, vz1, v1x_r, v1y_r, v1xy_r, v1z_r, s_v1, r_v1)
    for t in range(8):
        fk1[t] = jnp.where(lane < 64, b1[16 * t : 16 * t + 8, 0:128], b1[16 * t + 8 : 16 * t + 16, 0:128])
    zpack1(lambda x: b1[8 * x : 8 * x + 8, 128:256], fz1)
    start(ef1)
    arrive(ef1)
    unpack1(fk1, f1x_r, f1y_r, f1xy_r, f1z_r, clean(lev1), 2)
    smooth_down(lev1)
    for x in range(8):
        s1[8 * x : 8 * x + 8, :] = residual(lev1, 6 + 2 * x) + residual(lev1, 7 + 2 * x)

    rows = []
    for y in range(4):
        a = s1[pl.ds(2 * y, 8, stride=8), :] + s1[pl.ds(2 * y + 1, 8, stride=8), :]
        rows.append(split_rows(a, (row + y) % 2 == 0))
    b2 = moved(jnp.concatenate(rows, axis=0), to_pairs2)

    def copies2(t, tr, ss, rs):
        out = []
        for k, d in enumerate(D44):
            dst = tr.at[D44.index(neg(d))]
            out.append((d, pltpu.make_async_remote_copy(t, dst, ss.at[k], rs.at[k], at(d), MESH)))
        return out

    def unpack2(own, tr, which, put, colours):
        part = lane % 32
        for ny in which:
            if ny == -2:
                ys = [(i, 1 + i) for i in range(3)]
            elif ny == 2:
                ys = [(15 + i, i) for i in range(3)]
            else:
                ys = [(7 + 4 * ny + i, i) for i in range(4)]
            for nx in (-1, 0, 1):
                mid = own[...] if (nx, ny) == (0, 0) else tr[D44.index((nx, ny, 0))]
                low, high = tr[D44.index((nx, ny, -1))], tr[D44.index((nx, ny, 1))]
                for colour in range(colours):
                    a = roll(mid, -16 * colour, 1)
                    b = roll(high, 16 - 16 * colour, 1)
                    c = roll(low, 112 - 16 * colour, 1)
                    mixed = jnp.where(part < 16, a, jnp.where(part < 24, b, c))
                    for e, y in ys:
                        put(colour, e, 16 + 8 * nx, 8, roll(mixed, -32 * y, 1))

    ef2 = copies2(ft2, f2_r, s_f2, r_f2)
    ev2 = copies2(vt2, v2_r, s_v2, r_v2)
    acc = b2[0:8]
    for y in range(1, 4):
        acc = jnp.where(lane // 32 == y, b2[8 * y : 8 * y + 8], acc)
    ft2[...] = acc
    start(ef2)
    arrive([(d, c) for d, c in ef2 if abs(d[1]) < 2])
    unpack2(ft2, f2_r, (-1, 0, 1), clean(lev2), 2)
    smooth_down(lev2)

    for y in range(2):
        s2[8 * y : 8 * y + 8, :] = residual(lev2, 7 + 2 * y) + residual(lev2, 8 + 2 * y)
    a3 = s2[pl.ds(0, 8, stride=2), :] + s2[pl.ds(1, 8, stride=2), :]
    a3 = jnp.where(lane < 16, 0.5 * a3, 0.0)
    a3 = pltpu.roll(a3, 0, 1, stride=16, stride_axis=0)
    a3 = jnp.sum(a3, axis=0, keepdims=True)
    t3[...] = jnp.where(row == iy, a3, 0.0)

    egy, egz, egx = [], [], []
    for k in range(1, NGY):
        peer = (ix, lax.rem(iy + k, NGY), iz)
        egy.append(pltpu.make_async_remote_copy(t3, gy_r.at[k - 1], s_g.at[k - 1], r_g.at[k - 1], peer, MESH))
    for k in range(1, NGZ):
        peer = (ix, iy, lax.rem(iz + k, NGZ))
        n = 6 + k
        egz.append(pltpu.make_async_remote_copy(gzb.at[iz], gzb.at[iz], s_g.at[n], r_g.at[n], peer, MESH))
    for k in range(1, NGX):
        peer = (lax.rem(ix + k, NGX), iy, iz)
        n = 9 + k
        egx.append(pltpu.make_async_remote_copy(gzb, gxb.at[ix], s_g.at[n], r_g.at[n], peer, MESH))

    for c in egy:
        c.start()
    acc = jnp.zeros((8, 128), F32)
    for y in range(4):
        acc = jnp.where(lane // 32 == y, roll(vb2[7 + y, 16:24, :], 32 * y, 1), acc)
    vt2[...] = acc
    for t in range(8):
        vk1[t] = jnp.where(lane < 64, vb1[6 + 2 * t, 16:24, :], roll(vb1[7 + 2 * t, 16:24, :], 64, 1))
    zpack1(lambda x: vb1[6 + x, 16:24, :], vz1)
    pack0(lambda x: vb0[4 + x, 8:24, :], vy0, vz0)
    arrive([(d, c) for d, c in ef2 if abs(d[1]) == 2])
    unpack2(ft2, f2_r, (-2, 2), clean(lev2), 2)
    for c in egy:
        c.wait_recv()
    line = t3[...]
    for k in range(NGY - 1):
        line = line + gy_r[k]
    gzb[iz] = line
    for c in egz:
        c.start()
    for c in egz:
        c.wait_recv()
    for c in egx:
        c.start()
    start(ev2)
    start(ev1)
    start(ev0)
    gxb[ix] = gzb[...]
    for c in egx:
        c.wait_recv()

    for gx in range(NGX):
        for xl in range(4):
            acc = jnp.zeros((8, 128), F32)
            for gz in range(NGZ):
                acc = jnp.where((lane % 64) // 16 == gz, roll(gxb[gx, gz], (gz - xl) * 16, 1), acc)
            g3[4 * gx + xl] = acc

    zl = lane % 64
    w_lo = jnp.where(zl == 0, 0.0, BETA1)
    w_hi = jnp.where(zl == 63, 0.0, BETA1)
    y_edge = jnp.where(((row == 0) & (lane < 64)) | ((row == 7) & (lane >= 64)), 0.0, 1.0)
    par3 = (lane // 64 + lane) & 1
    colours3 = (par3 == 0, par3 == 1)

    def sum3(x):
        c = v3[x + 4]
        a = roll(c, 64, 1)
        w = jnp.where(lane < 64, roll(a, 1, 0), roll(a, -1, 0)) * y_edge
        s = (v3[x + 3] + v3[x + 5]) + (a + w)
        return c, s + (roll(c, 1, 1) * w_lo + roll(c, -1, 1) * w_hi)

    def half3(colour):
        for j in range(4):
            done = []
            for x in range(8 * j, 8 * j + 8):
                c, s = sum3(x)
                done.append(jnp.where(colours3[(x + colour) % 2], (g3[x] + s) * INV, c))
            for u in range(8):
                v3[8 * j + u + 4] = done[u]

    for x in range(32):
        v3[x + 4] = jnp.where(colours3[x % 2], g3[x] * INV, 0.0)
    half3(1)
    half3(0)
    half3(1)

    def small(g, level):
        n = len(g)
        dz, dy = 2 ** (level - 3), 2 ** (level - 4)
        lo = jnp.where(zl < dz, 0.0, BETA1)
        hi = jnp.where(zl >= 64 - dz, 0.0, BETA1)
        ylo = jnp.where(row < dy, 0.0, 1.0)
        yhi = jnp.where(row >= 8 - dy, 0.0, 1.0)
        par = (row // dy + zl // dz) & 1
        colours = (par == 0, par == 1)

        def total(v, x):
            c = v[x]
            s = roll(c, dz, 1) * lo + roll(c, -dz, 1) * hi
            s = s + (roll(c, dy, 0) * ylo + roll(c, -dy, 0) * yhi)
            if x > 0:
                s = s + v[x - 1]
            if x < n - 1:
                s = s + v[x + 1]
            return s

        def sweep(v, colour):
            return [
                jnp.where(colours[(x + colour) % 2], (g[x] + total(v, x)) * INV, v[x]) for x in range(n)
            ]

        v = [jnp.where(colours[x % 2], g[x] * INV, 0.0) for x in range(n)]
        v = sweep(v, 1)
        if level == 6:
            for _ in range(CSWEEPS - 1):
                v = sweep(sweep(v, 0), 1)
            return v
        v = sweep(sweep(v, 0), 1)
        r = [g[x] - (CENTRE * v[x] - total(v, x)) for x in range(n)]
        coarse = []
        for x in range(n // 2):
            t = r[2 * x] + r[2 * x + 1]
            t = t + jnp.where((row // dy) % 2 == 0, roll(t, -dy, 0), roll(t, dy, 0))
            t = t + jnp.where((zl // dz) % 2 == 0, roll(t, -dz, 1), roll(t, dz, 1))
            coarse.append(0.5 * t)
        e = small(coarse, level + 1)
        v = [v[x] + e[x // 2] for x in range(n)]
        for _ in range(2):
            v = sweep(sweep(v, 0), 1)
        return v

    def resid3(x):
        c, s = sum3(x)
        return g3[x] - (CENTRE * c - s)

    g4 = []
    for x in range(16):
        t = resid3(2 * x) + resid3(2 * x + 1)
        t = t + roll(t, 64, 1)
        t = t + jnp.where(lane % 2 == 0, roll(t, -1, 1), roll(t, 1, 1))
        g4.append(0.5 * t)
    e4 = small(g4, 4)
    for x in range(32):
        v3[4 + x] = v3[4 + x] + e4[x // 2]
    for _ in range(2):
        half3(0)
        half3(1)

    for x in range(12):
        e = v3[4 * ix + x]
        for yl in range(2):
            tmp2[yl, 16 + 8 * x : 24 + 8 * x, :] = pltpu.roll(e, (128 - 16 * iz + 64 * yl) % 128, 1)
    for j in range(10):
        e = tmp2[j % 2, pl.ds(16 + iy - 2 + j // 2, 12, stride=8), :]
        pe2[j, pl.ds(8, 12, stride=2), :] = e
        pe2[j, pl.ds(9, 12, stride=2), :] = e
    arrive(ev2)
    sent(ev2)
    add2 = corrected(lev2, lambda i, dst, num: pe2[(i + 1) // 2, dst : dst + num, :])
    unpack2(vt2, v2_r, (-2, -1, 0, 1, 2), add2, 1)
    half(lev2, 1, 17, True)
    half(lev2, 2, 16, False)
    half(lev2, 3, 15, True)
    half(lev2, 4, 14, False)

    def cells(level, i, a, b):
        even = level.even(i, a, b)
        r, k = level.vr[i, a:b, :], level.vb[i, a:b, :]
        return jnp.concatenate([jnp.where(even, r, k), jnp.where(even, k, r)], axis=1)

    rows = [cells(lev2, i, 8, 32) for i in range(3, 15)]
    tmp1[...] = moved(jnp.concatenate(rows, axis=0), from_pairs)
    for k in range(14):
        e = tmp1[pl.ds(5 + k, 12, stride=24), :]
        pe1[k, pl.ds(8, 12, stride=2), :] = e
        pe1[k, pl.ds(9, 12, stride=2), :] = e
    arrive(ev1)
    sent(ev1)
    add1 = corrected(lev1, lambda i, dst, num: pe1[i // 2, dst : dst + num, :])
    unpack1(vk1, v1x_r, v1y_r, v1xy_r, v1z_r, add1, 1)
    half(lev1, 1, 27, True)
    half(lev1, 2, 26, False)
    half(lev1, 3, 25, True)
    half(lev1, 4, 24, False)

    rows = [cells(lev1, i, 14, 30) for i in range(4, 24)]
    u1 = moved(jnp.concatenate(rows, axis=0), from_pairs)
    for k in range(20):
        e = u1[16 * k : 16 * k + 12]
        pe0[k, pl.ds(4, 12, stride=2), :] = e
        pe0[k, pl.ds(5, 12, stride=2), :] = e
    arrive(ev0)
    sent(ev0)
    add0 = corrected(lev0, lambda i, dst, num: pe0[i // 2, dst : dst + num, :])
    unpack0(lambda x: vb0[4 + x, 8:24, :], vx_r, vy_r, vxy_r, vz_r, add0, 1)
    half(lev0, 1, 39, True)
    half(lev0, 2, 38, False)
    half(lev0, 3, 37, True)
    half(lev0, 4, 36, False, (8, 24))

    stores = []
    for part in range(4):
        rows = [cells(lev0, 4 + x, 8, 24) for x in range(8 * part, 8 * part + 8)]
        out[pl.ds(8 * part, 8)] = moved(jnp.concatenate(rows, axis=0), to_cells).reshape(8, 16, 128)
        here = pl.ds(8 * part, 8)
        stores.append(pltpu.make_async_copy(out.at[here], out_hbm.at[here], io_sem.at[1 + part]))
        stores[-1].start()
    for e in (ef0, ef1, ef2):
        sent(e)
    for c in egy + egz + egx:
        c.wait_send()
    for s in stores:
        s.wait()


def on_device(density):
    def vmem(*shape):
        return pltpu.VMEM(shape, F32)

    coef = vmem(2, 32, 128)
    level0 = [vmem(BX, BY, BZ)] * 2 + [vmem(40, 32, 128)] * 4 + [coef, vmem(16, 16, 128), vmem(20, 32, 128)]
    level0 += [vmem(BX, BY, BZ)]
    level1 = [vmem(28, 40, 128)] * 4 + [coef, vmem(64, 128), vmem(14, 32, 128), vmem(288, 128)]
    level2 = [vmem(18, 40, 128)] * 4 + [coef, vmem(16, 128), vmem(10, 32, 128), vmem(2, 128, 128)]
    packs = [vmem(2, 16, 8, 128), vmem(2, 16, 128)] * 2 + [vmem(8, 8, 128), vmem(2, 8, 128)] * 2
    packs += [vmem(8, 128)] * 2
    recv0 = [vmem(2, 4, 16, 128), vmem(2, 16, 8, 128), vmem(4, 2, 8, 128), vmem(18, 16, 128)] * 2
    recv1 = [vmem(2, 3, 8, 128), vmem(2, 8, 8, 128), vmem(4, 3, 8, 128), vmem(18, 8, 128)] * 2
    recv2 = [vmem(44, 8, 128)] * 2
    gather = [vmem(8, 128), vmem(7, 8, 128), vmem(4, 8, 128), vmem(8, 4, 8, 128), vmem(32, 8, 128), vmem(40, 8, 128)]
    dma = pltpu.SemaphoreType.DMA
    sems = [dma((5,))] + [dma((26,))] * 8 + [dma((44,))] * 4 + [dma((17,))] * 2
    return pl.pallas_call(
        kernel,
        out_shape=jax.ShapeDtypeStruct((BX, BY, BZ), F32),
        in_specs=[pl.BlockSpec(memory_space=pl.ANY)],
        out_specs=pl.BlockSpec(memory_space=pl.ANY),
        scratch_shapes=level0 + level1 + level2 + packs + recv0 + recv1 + recv2 + gather + sems,
        compiler_params=pltpu.CompilerParams(
            collective_id=0, has_side_effects=True, vmem_limit_bytes=48 * 1024 * 1024
        ),
    )(density)


def solution(mesh):
    spec = P("gx", "gy", "gz")
    return jax.shard_map(on_device, mesh=mesh, in_specs=(spec,), out_specs=spec, check_vma=False)
```

time: 80.3 us -> 54.7 us (0.68)
  Pallas kernels: 78.5 us -> 52.9 us
    pallas_call x1, Pallas kernels: 78.5 us -> 52.9 us  [on_device(): pl.pallas_call(kernel, out_shape=jax.ShapeDtypeStruct((BX, BY, BZ), F32),...]
where the time goes in v2:
time: 54.7 us; the launch traced here: 54.6 us
  Pallas kernels  52.9 us (97%)
  local copies, waits for them, and re-layouts  1.65 us (3%)
    pallas_call x1, Pallas kernels, on_device(): pl.pallas_call(kernel, out_shape=jax.ShapeDtypeStruct((BX, BY, BZ), F32),...  52.9 us
    unnamed x3, local copies, waits for them, and re-layouts  1.65 us

profile of v2, /device:TPU:1, one launch (start us, length us, event | category | flops | bytes accessed | tf_op | source)
XLA Modules:
  0.0 54.6 jit_solution(10924583595568113925)
XLA Ops:
  0.0 0.0 copy-start
  0.0 0.9 %copy-done = f32[32,16,128]{2,1,0:T(8,128)S(1)} copy-done((f32[32,16,128]{2,1,0:T(8,128)S(1)}, f32[32,16,128]{2,1,0:T(8,128)}, u32[]{:S(2)}) %copy-start) | copy-done | bytes 262168
  1.0 52.9 %shard_map.17 = f32[32,16,128]{2,1,0:T(8,128)S(1)} custom-call(f32[32,16,128]{2,1,0:T(8,128)S(1)} %copy-done), custom_call_target="tpu_custom_call" | custom-call | tf_op jit(solution)/shard_map/pallas_call | solution.py:677
  53.9 0.7 %copy.3 = f32[32,16,128]{2,1,0:T(8,128)} copy(f32[32,16,128]{2,1,0:T(8,128)S(1)} %shard_map.17) | data formatting | bytes 524288
Async XLA Ops:
  0.0 0.9 %copy-start = (f32[32,16,128]{2,1,0:T(8,128)S(1)}, f32[32,16,128]{2,1,0:T(8,128)}, u32[]{:S(2)}) copy-start(f32[32,16,128]{2,1,0:T(8,128)} %f_hbm.1) | copy-start | bytes 786436

commit v3 on v2

--- a/solution.py
+++ b/solution.py
@@ -19,7 +19,8 @@
 INV = 1.0 / CENTRE
 
 D26 = [d for d in itertools.product((-1, 0, 1), repeat=3) if d != (0, 0, 0)]
-D44 = [d for d in itertools.product((-1, 0, 1), (-2, -1, 0, 1, 2), (-1, 0, 1)) if d != (0, 0, 0)]
+D26.sort(key=lambda d: -sum(map(abs, d)))
+D44 = D26 + [d for d in itertools.product((-1, 0, 1), (-2, 2), (-1, 0, 1))]
 XY4 = [(-1, -1), (-1, 1), (1, -1), (1, 1)]
 Z18 = [d for d in D26 if d[2] != 0]
 
@@ -55,16 +56,16 @@
 
 
 def kernel(
-    f_hbm, out_hbm,
-    f0, p0, fr0, fb0, vr0, vb0, k0, s0, pe0, out,
+    f_hbm, out,
+    f0, p0, fr0, fb0, vr0, vb0, k0, s0, pe0,
     fr1, fb1, vr1, vb1, k1, s1, pe1, tmp1,
     fr2, fb2, vr2, vb2, k2, s2, pe2, tmp2,
-    fy0, fz0, vy0, vz0, fk1, fz1, vk1, vz1, ft2, vt2,
+    fy0, fz0, vy0, vz0, vx0, fk1, fz1, vk1, vz1, ft2, vt2,
     fx_r, fy_r, fxy_r, fz_r, vx_r, vy_r, vxy_r, vz_r,
     f1x_r, f1y_r, f1xy_r, f1z_r, v1x_r, v1y_r, v1xy_r, v1z_r,
     f2_r, v2_r,
     t3, gy_r, gzb, gxb, g3, v3,
-    io_sem, s_f0, r_f0, s_v0, r_v0, s_f1, r_f1, s_v1, r_v1, s_f2, r_f2, s_v2, r_v2, s_g, r_g,
+    spare, tok, tok4, io_sem, s_all, r_f0, r_v0, r_f1, r_v1, r_f2, r_f2b, r_v2, r_gy, r_gz, r_gx,
 ):
     ix, iy, iz = lax.axis_index("gx"), lax.axis_index("gy"), lax.axis_index("gz")
 
@@ -79,12 +80,12 @@
             jnp.clip(iz + n[2], 0, NGZ - 1),
         )
 
-    load = pltpu.make_async_copy(f_hbm, f0, io_sem.at[0])
+    load = pltpu.make_async_copy(f_hbm, f0, io_sem)
     load.start()
 
     barrier = pltpu.get_barrier_semaphore()
     count = 0
-    for d in D44:
+    for d in D26:
         ok = there(d)
         count = count + ok.astype(jnp.int32)
 
@@ -92,32 +93,17 @@
         def _(d=d):
             pl.semaphore_signal(barrier, inc=1, device_id=at(d), device_id_type=MESH)
 
-    lines = []
-    for k in range(1, NGY):
-        lines.append((ix, lax.rem(iy + k, NGY), iz))
-    for k in range(1, NGZ):
-        lines.append((ix, iy, lax.rem(iz + k, NGZ)))
-    for k in range(1, NGX):
-        lines.append((lax.rem(ix + k, NGX), iy, iz))
-    for peer in lines:
-        pl.semaphore_signal(barrier, inc=1, device_id=peer, device_id_type=MESH)
+    def token(sem, reach):
+        for d in ((-reach, 0, 0), (reach, 0, 0), (0, -reach, 0), (0, reach, 0)):
+            @pl.when(there(d))
+            def _(d=d):
+                pl.semaphore_signal(sem, inc=1, device_id=at(d), device_id_type=MESH)
 
     lane = iota((8, 128), 1)
     row = iota((8, 128), 0)
     lane16 = iota((16, 128), 1)
     r32, l32 = iota((32, 128), 0), iota((32, 128), 1)
     signed = jnp.where(l32 < 96, l32, l32 - 128)
-
-    def fill(ref, halo, pairs, start_pairs, total_pairs, rows_at, total_rows):
-        zp = start_pairs + signed
-        ok = (signed >= -halo) & (signed < pairs + halo) & (zp >= 0) & (zp < total_pairs)
-        ok = ok & (rows_at >= 0) & (rows_at < total_rows)
-        ref[0] = jnp.zeros((32, 128), F32)
-        ref[1] = jnp.where(ok, INV, 0.0)
-
-    fill(k0, 2, 64, iz * 64, NGZ * 64, iy * BY + r32 - 8, NGY * BY)
-    fill(k1, 3, 32, iz * 32, NGZ * 32, iy * 8 + r32 - 16, NGY * 8)
-    fill(k2, 4, 16, iz * 16, NGZ * 16, ix * 8 + r32 - 16, NGX * 8)
 
     class Level:
         def __init__(self, fr, fb, vr, vb, k, first, main, rows, window, odd, start, total):
@@ -176,19 +162,6 @@
         black = level.fb[i, a:b, :] - (CENTRE * vb - around(level, level.vr, i, a, b, False))
         return red + black
 
-    def zero(ref):
-        @pl.loop(0, ref.shape[0])
-        def _(i):
-            ref[i] = jnp.zeros(ref.shape[1:], F32)
-
-    for ref in (vr0, vb0, vr1, vb1, vr2, vb2, pe0, pe1, pe2, v3, tmp2):
-        zero(ref)
-
-    def splitter(total, where):
-        k, c = iota((256, total), 0), iota((256, total), 1)
-        z = k % 128
-        return z, (z + k // 128) % 2 == 0, c, where
-
     def split_rows(a, even):
         return jnp.concatenate([jnp.where(even, a, 0.0), jnp.where(even, 0.0, a)], axis=1)
 
@@ -198,14 +171,19 @@
 
     load.wait()
 
-    to_pairs = jnp.where(c128 == z256 // 2 + jnp.where(red256, 0, 64), 1.0, 0.0).astype(BF16)
+    kk2, cc2 = iota((256, 256), 0), iota((256, 256), 1)
+    same = kk2 // 128 == cc2 // 128
+    kk2, cc2 = kk2 % 128, cc2 % 128
+    to_pairs = jnp.where(same & (cc2 == kk2 // 2 + 64 * (kk2 % 2)), 1.0, 0.0).astype(BF16)
+    to_cells = jnp.where(same & (kk2 == cc2 // 2 + 64 * (cc2 % 2)), 1.0, 0.0).astype(BF16)
     for part in range(4):
         rows = []
-        for x in range(8 * part, 8 * part + 8):
-            rows.append(split_rows(f0[x], (iota((16, 128), 0) + x) % 2 == 0))
+        for x in range(8 * part, 8 * part + 8, 2):
+            rows.append(jnp.concatenate([f0[x], f0[x + 1]], axis=1))
         p = moved(jnp.concatenate(rows, axis=0), to_pairs)
         for x in range(8):
-            p0[8 * part + x] = p[16 * x : 16 * x + 16]
+            q = p[16 * (x // 2) : 16 * (x // 2) + 16, 128 * (x % 2) : 128 * (x % 2) + 128]
+            p0[8 * part + x] = jnp.where((iota((16, 128), 0) + x) % 2 == 0, q, roll(q, 64, 1))
 
     def pack0(plane, yp, zp):
         lo = jnp.zeros((16, 128), F32)
@@ -224,7 +202,7 @@
 
     def copies0(xs, yp, zp, xr, yr, xyr, zr, ss, rs):
         out = []
-        for k, d in enumerate(D26):
+        for d in D26:
             dx, dy, dz = d
             if dz == 0 and dy == 0:
                 s, t = xs(dx), xr.at[side(-dx)]
@@ -240,7 +218,7 @@
                 else:
                     rows = pl.ds(0 if dy < 0 else 8, 8)
                     s, t = zp.at[side(dz), rows], zr.at[slot, rows]
-            out.append((d, pltpu.make_async_remote_copy(s, t, ss.at[k], rs.at[k], at(d), MESH)))
+            out.append((d, pltpu.make_async_remote_copy(s, t, ss, rs, at(d), MESH)))
         return out
 
     def start(copies):
@@ -249,17 +227,31 @@
             def _(c=c):
                 c.start()
 
-    def arrive(copies):
-        for d, c in copies:
-            @pl.when(there(neg(d)))
-            def _(c=c):
-                c.wait_recv()
-
-    def sent(copies):
-        for d, c in copies:
-            @pl.when(there(d))
-            def _(c=c):
-                c.wait_send()
+    near_x = jnp.where((ix > 0) & (ix < NGX - 1), 2, 1)
+    near_z = jnp.where((iz > 0) & (iz < NGZ - 1), 2, 1)
+    near_y = jnp.where((iy > 0) & (iy < NGY - 1), 2, 1)
+    far_y = jnp.where((iy > 1) & (iy < NGY - 2), 2, 1)
+
+    def units0(x, y, y2, z):
+        return x * 8 + y * 16 + x * y * 2 + z * (2 + 2 * x + y + x * y)
+
+    def units1(x, y, y2, z):
+        return x * 3 + y * 8 + x * y * 3 + z * (1 + x) * (1 + y)
+
+    def units2(x, y, y2, z):
+        return (1 + x) * (1 + y) * (1 + z) - 1
+
+    def units2b(x, y, y2, z):
+        return (1 + x) * y2 * (1 + z)
+
+    def wait_units(sem, n):
+        pltpu.make_async_copy(spare.at[pl.ds(0, n)], spare.at[pl.ds(0, n)], sem).wait()
+
+    def arrive(sem, units):
+        for x, (y, y2), z in itertools.product((1, 2), ((1, 1), (2, 1), (2, 2)), (1, 2)):
+            @pl.when((near_x == x) & (near_y == y) & (far_y == y2) & (near_z == z))
+            def _(n=units(x, y, y2, z)):
+                wait_units(sem, n)
 
     def unpack0(own, xr, yr, xyr, zr, put, colours):
         for nx in (-1, 0, 1):
@@ -305,16 +297,35 @@
         return put
 
     ef0 = copies0(
-        lambda dx: p0.at[pl.ds(0 if dx < 0 else 28, 4)], fy0, fz0, fx_r, fy_r, fxy_r, fz_r, s_f0, r_f0
+        lambda dx: p0.at[pl.ds(0 if dx < 0 else 28, 4)], fy0, fz0, fx_r, fy_r, fxy_r, fz_r, s_all, r_f0
     )
     ev0 = copies0(
-        lambda dx: vb0.at[pl.ds(4 if dx < 0 else 32, 4), pl.ds(8, BY), :],
-        vy0, vz0, vx_r, vy_r, vxy_r, vz_r, s_v0, r_v0,
+        lambda dx: vx0.at[side(dx)],
+        vy0, vz0, vx_r, vy_r, vxy_r, vz_r, s_all, r_v0,
     )
 
     pack0(lambda x: p0[x], fy0, fz0)
-    pl.semaphore_wait(barrier, count + len(lines))
+    pl.semaphore_wait(barrier, count)
     start(ef0)
+
+    def fill(ref, halo, pairs, start_pairs, total_pairs, rows_at, total_rows):
+        zp = start_pairs + signed
+        ok = (signed >= -halo) & (signed < pairs + halo) & (zp >= 0) & (zp < total_pairs)
+        ok = ok & (rows_at >= 0) & (rows_at < total_rows)
+        ref[0] = jnp.zeros((32, 128), F32)
+        ref[1] = jnp.where(ok, INV, 0.0)
+
+    fill(k0, 2, 64, iz * 64, NGZ * 64, iy * BY + r32 - 8, NGY * BY)
+    fill(k1, 3, 32, iz * 32, NGZ * 32, iy * 8 + r32 - 16, NGY * 8)
+    fill(k2, 4, 16, iz * 16, NGZ * 16, ix * 8 + r32 - 16, NGX * 8)
+
+    def zero(ref):
+        @pl.loop(0, ref.shape[0])
+        def _(i):
+            ref[i] = jnp.zeros(ref.shape[1:], F32)
+
+    for ref in (vr0, vb0, vr1, vb1, vr2, vb2, pe0, pe1, pe2, v3, tmp2):
+        zero(ref)
 
     split1 = iota((256, 256), 1)
     k1i = iota((256, 256), 0)
@@ -326,12 +337,12 @@
     to_pairs2 = jnp.where(
         (z256 < 32) & (c128 % 32 == z256 // 2 + jnp.where(red256, 0, 16)), 0.5, 0.0
     ).astype(BF16)
-    csign = jnp.where(c128 < 96, c128, c128 - 128)
-    wanted = ((csign + 128) // 2 - 64) % 128 + 128 * ((csign + 128) % 2)
-    from_pairs = jnp.where((k256 == wanted) & (csign >= -4) & (csign < 68), 1.0, 0.0).astype(BF16)
-    to_cells = jnp.where(k256 == c128 // 2 + 128 * (c128 % 2), 1.0, 0.0).astype(BF16)
-
-    arrive(ef0)
+    csign = jnp.where(cc2 < 96, cc2, cc2 - 128)
+    wanted = ((csign + 128) // 2 - 64 + 64 * (csign % 2)) % 128
+    from_pairs = jnp.where(same & (kk2 == wanted) & (csign >= -4) & (csign < 68), 1.0, 0.0).astype(BF16)
+
+    arrive(r_f0, units0)
+    token(tok, 2)
     unpack0(lambda x: p0[x], fx_r, fy_r, fxy_r, fz_r, clean(lev0), 2)
     smooth_down(lev0)
     for x in range(16):
@@ -356,7 +367,7 @@
 
     def copies1(pk, zp, xr, yr, xyr, zr, ss, rs):
         out = []
-        for k, d in enumerate(D26):
+        for d in D26:
             dx, dy, dz = d
             if dz == 0 and dx == 0:
                 s, t = pk, yr.at[side(-dy)]
@@ -365,7 +376,7 @@
                 t = xr.at[side(-dx)] if dy == 0 else xyr.at[XY4.index((-dx, -dy))]
             else:
                 s, t = zp.at[side(dz)], zr.at[Z18.index(neg(d))]
-            out.append((d, pltpu.make_async_remote_copy(s, t, ss.at[k], rs.at[k], at(d), MESH)))
+            out.append((d, pltpu.make_async_remote_copy(s, t, ss, rs, at(d), MESH)))
         return out
 
     def unpack1(pk, xr, yr, xyr, zr, put, colours):
@@ -384,13 +395,15 @@
                     c = roll(low, 125 - 3 * x - 64 * colour, 1)
                     put(colour, xe, 16 + 8 * ny, 8, jnp.where(lane < 32, a, jnp.where(lane < 64, b, c)))
 
-    ef1 = copies1(fk1, fz1, f1x_r, f1y_r, f1xy_r, f1z_r, s_f1, r_f1)
-    ev1 = copies1(vk1, vz1, v1x_r, v1y_r, v1xy_r, v1z_r, s_v1, r_v1)
+    ef1 = copies1(fk1, fz1, f1x_r, f1y_r, f1xy_r, f1z_r, s_all, r_f1)
+    ev1 = copies1(vk1, vz1, v1x_r, v1y_r, v1xy_r, v1z_r, s_all, r_v1)
     for t in range(8):
         fk1[t] = jnp.where(lane < 64, b1[16 * t : 16 * t + 8, 0:128], b1[16 * t + 8 : 16 * t + 16, 0:128])
     zpack1(lambda x: b1[8 * x : 8 * x + 8, 128:256], fz1)
     start(ef1)
-    arrive(ef1)
+    arrive(r_f1, units1)
+    pl.semaphore_wait(tok, jnp.where((ix > 1) & (ix < NGX - 2), 2, 1) + far_y)
+    token(tok4, 4)
     unpack1(fk1, f1x_r, f1y_r, f1xy_r, f1z_r, clean(lev1), 2)
     smooth_down(lev1)
     for x in range(8):
@@ -402,11 +415,11 @@
         rows.append(split_rows(a, (row + y) % 2 == 0))
     b2 = moved(jnp.concatenate(rows, axis=0), to_pairs2)
 
-    def copies2(t, tr, ss, rs):
+    def copies2(t, tr, ss, rs, directions):
         out = []
-        for k, d in enumerate(D44):
+        for d in directions:
             dst = tr.at[D44.index(neg(d))]
-            out.append((d, pltpu.make_async_remote_copy(t, dst, ss.at[k], rs.at[k], at(d), MESH)))
+            out.append((d, pltpu.make_async_remote_copy(t, dst, ss, rs, at(d), MESH)))
         return out
 
     def unpack2(own, tr, which, put, colours):
@@ -429,14 +442,15 @@
                     for e, y in ys:
                         put(colour, e, 16 + 8 * nx, 8, roll(mixed, -32 * y, 1))
 
-    ef2 = copies2(ft2, f2_r, s_f2, r_f2)
-    ev2 = copies2(vt2, v2_r, s_v2, r_v2)
+    ef2 = copies2(ft2, f2_r, s_all, r_f2, D26)
+    ef2b = copies2(ft2, f2_r, s_all, r_f2b, D44[26:])
+    ev2 = copies2(vt2, v2_r, s_all, r_v2, D44)
     acc = b2[0:8]
     for y in range(1, 4):
         acc = jnp.where(lane // 32 == y, b2[8 * y : 8 * y + 8], acc)
     ft2[...] = acc
     start(ef2)
-    arrive([(d, c) for d, c in ef2 if abs(d[1]) < 2])
+    arrive(r_f2, units2)
     unpack2(ft2, f2_r, (-1, 0, 1), clean(lev2), 2)
     smooth_down(lev2)
 
@@ -451,18 +465,18 @@
     egy, egz, egx = [], [], []
     for k in range(1, NGY):
         peer = (ix, lax.rem(iy + k, NGY), iz)
-        egy.append(pltpu.make_async_remote_copy(t3, gy_r.at[k - 1], s_g.at[k - 1], r_g.at[k - 1], peer, MESH))
+        egy.append(pltpu.make_async_remote_copy(t3, gy_r.at[k - 1], s_all, r_gy, peer, MESH))
     for k in range(1, NGZ):
         peer = (ix, iy, lax.rem(iz + k, NGZ))
-        n = 6 + k
-        egz.append(pltpu.make_async_remote_copy(gzb.at[iz], gzb.at[iz], s_g.at[n], r_g.at[n], peer, MESH))
+        egz.append(pltpu.make_async_remote_copy(gzb.at[iz], gzb.at[iz], s_all, r_gz, peer, MESH))
     for k in range(1, NGX):
         peer = (lax.rem(ix + k, NGX), iy, iz)
-        n = 9 + k
-        egx.append(pltpu.make_async_remote_copy(gzb, gxb.at[ix], s_g.at[n], r_g.at[n], peer, MESH))
-
+        egx.append(pltpu.make_async_remote_copy(gzb, gxb.at[ix], s_all, r_gx, peer, MESH))
+
+    pl.semaphore_wait(tok4, 2)
     for c in egy:
         c.start()
+    start(ef2b)
     acc = jnp.zeros((8, 128), F32)
     for y in range(4):
         acc = jnp.where(lane // 32 == y, roll(vb2[7 + y, 16:24, :], 32 * y, 1), acc)
@@ -471,26 +485,26 @@
         vk1[t] = jnp.where(lane < 64, vb1[6 + 2 * t, 16:24, :], roll(vb1[7 + 2 * t, 16:24, :], 64, 1))
     zpack1(lambda x: vb1[6 + x, 16:24, :], vz1)
     pack0(lambda x: vb0[4 + x, 8:24, :], vy0, vz0)
-    arrive([(d, c) for d, c in ef2 if abs(d[1]) == 2])
+    for x in range(4):
+        vx0[0, x] = vb0[4 + x, 8:24, :]
+        vx0[1, x] = vb0[32 + x, 8:24, :]
+    arrive(r_f2b, units2b)
     unpack2(ft2, f2_r, (-2, 2), clean(lev2), 2)
-    for c in egy:
-        c.wait_recv()
+    wait_units(r_gy, 7)
     line = t3[...]
     for k in range(NGY - 1):
         line = line + gy_r[k]
     gzb[iz] = line
     for c in egz:
         c.start()
-    for c in egz:
-        c.wait_recv()
+    wait_units(r_gz, 3)
     for c in egx:
         c.start()
     start(ev2)
     start(ev1)
     start(ev0)
     gxb[ix] = gzb[...]
-    for c in egx:
-        c.wait_recv()
+    wait_units(r_gx, 28)
 
     for gx in range(NGX):
         for xl in range(4):
@@ -598,8 +612,7 @@
         e = tmp2[j % 2, pl.ds(16 + iy - 2 + j // 2, 12, stride=8), :]
         pe2[j, pl.ds(8, 12, stride=2), :] = e
         pe2[j, pl.ds(9, 12, stride=2), :] = e
-    arrive(ev2)
-    sent(ev2)
+    arrive(r_v2, lambda *c: units2(*c) + units2b(*c))
     add2 = corrected(lev2, lambda i, dst, num: pe2[(i + 1) // 2, dst : dst + num, :])
     unpack2(vt2, v2_r, (-2, -1, 0, 1, 2), add2, 1)
     half(lev2, 1, 17, True)
@@ -610,16 +623,27 @@
     def cells(level, i, a, b):
         even = level.even(i, a, b)
         r, k = level.vr[i, a:b, :], level.vb[i, a:b, :]
-        return jnp.concatenate([jnp.where(even, r, k), jnp.where(even, k, r)], axis=1)
-
-    rows = [cells(lev2, i, 8, 32) for i in range(3, 15)]
-    tmp1[...] = moved(jnp.concatenate(rows, axis=0), from_pairs)
+        first, second = jnp.where(even, r, k), roll(jnp.where(even, k, r), 64, 1)
+        lanes = iota((b - a, 128), 1)
+        if level is lev0:
+            return jnp.where(lanes < 64, first, second)
+        return jnp.where((lanes < 40) | (lanes >= 104), first, second)
+
+    def merged(level, planes, a, b, matrix):
+        rows = []
+        for i in range(0, len(planes), 2):
+            rows.append(jnp.concatenate([cells(level, j, a, b) for j in planes[i : i + 2]], axis=1))
+        u = moved(jnp.concatenate(rows, axis=0), matrix)
+        n = b - a
+        return [u[n * (i // 2) : n * (i // 2) + n, 128 * (i % 2) : 128 * (i % 2) + 128] for i in range(len(planes))]
+
+    for i, e in enumerate(merged(lev2, range(3, 15), 8, 32, from_pairs)):
+        tmp1[24 * i : 24 * i + 24, :] = e
     for k in range(14):
         e = tmp1[pl.ds(5 + k, 12, stride=24), :]
         pe1[k, pl.ds(8, 12, stride=2), :] = e
         pe1[k, pl.ds(9, 12, stride=2), :] = e
-    arrive(ev1)
-    sent(ev1)
+    arrive(r_v1, units1)
     add1 = corrected(lev1, lambda i, dst, num: pe1[i // 2, dst : dst + num, :])
     unpack1(vk1, v1x_r, v1y_r, v1xy_r, v1z_r, add1, 1)
     half(lev1, 1, 27, True)
@@ -627,14 +651,11 @@
     half(lev1, 3, 25, True)
     half(lev1, 4, 24, False)
 
-    rows = [cells(lev1, i, 14, 30) for i in range(4, 24)]
-    u1 = moved(jnp.concatenate(rows, axis=0), from_pairs)
-    for k in range(20):
-        e = u1[16 * k : 16 * k + 12]
+    for k, e in enumerate(merged(lev1, range(4, 24), 14, 30, from_pairs)):
+        e = e[0:12]
         pe0[k, pl.ds(4, 12, stride=2), :] = e
         pe0[k, pl.ds(5, 12, stride=2), :] = e
-    arrive(ev0)
-    sent(ev0)
+    arrive(r_v0, units0)
     add0 = corrected(lev0, lambda i, dst, num: pe0[i // 2, dst : dst + num, :])
     unpack0(lambda x: vb0[4 + x, 8:24, :], vx_r, vy_r, vxy_r, vz_r, add0, 1)
     half(lev0, 1, 39, True)
@@ -642,19 +663,11 @@
     half(lev0, 3, 37, True)
     half(lev0, 4, 36, False, (8, 24))
 
-    stores = []
     for part in range(4):
-        rows = [cells(lev0, 4 + x, 8, 24) for x in range(8 * part, 8 * part + 8)]
-        out[pl.ds(8 * part, 8)] = moved(jnp.concatenate(rows, axis=0), to_cells).reshape(8, 16, 128)
-        here = pl.ds(8 * part, 8)
-        stores.append(pltpu.make_async_copy(out.at[here], out_hbm.at[here], io_sem.at[1 + part]))
-        stores[-1].start()
-    for e in (ef0, ef1, ef2):
-        sent(e)
-    for c in egy + egz + egx:
-        c.wait_send()
-    for s in stores:
-        s.wait()
+        planes = range(4 + 8 * part, 12 + 8 * part)
+        for x, e in enumerate(merged(lev0, planes, 8, 24, to_cells)):
+            out[8 * part + x] = e
+    arrive(s_all, lambda *c: 2 * (units0(*c) + units1(*c) + units2(*c) + units2b(*c)) + 38)
 
 
 def on_device(density):
@@ -663,22 +676,22 @@
 
     coef = vmem(2, 32, 128)
     level0 = [vmem(BX, BY, BZ)] * 2 + [vmem(40, 32, 128)] * 4 + [coef, vmem(16, 16, 128), vmem(20, 32, 128)]
-    level0 += [vmem(BX, BY, BZ)]
     level1 = [vmem(28, 40, 128)] * 4 + [coef, vmem(64, 128), vmem(14, 32, 128), vmem(288, 128)]
     level2 = [vmem(18, 40, 128)] * 4 + [coef, vmem(16, 128), vmem(10, 32, 128), vmem(2, 128, 128)]
-    packs = [vmem(2, 16, 8, 128), vmem(2, 16, 128)] * 2 + [vmem(8, 8, 128), vmem(2, 8, 128)] * 2
+    packs = [vmem(2, 16, 8, 128), vmem(2, 16, 128)] * 2 + [vmem(2, 4, 16, 128)] + [vmem(8, 8, 128), vmem(2, 8, 128)] * 2
     packs += [vmem(8, 128)] * 2
     recv0 = [vmem(2, 4, 16, 128), vmem(2, 16, 8, 128), vmem(4, 2, 8, 128), vmem(18, 16, 128)] * 2
     recv1 = [vmem(2, 3, 8, 128), vmem(2, 8, 8, 128), vmem(4, 3, 8, 128), vmem(18, 8, 128)] * 2
     recv2 = [vmem(44, 8, 128)] * 2
     gather = [vmem(8, 128), vmem(7, 8, 128), vmem(4, 8, 128), vmem(8, 4, 8, 128), vmem(32, 8, 128), vmem(40, 8, 128)]
     dma = pltpu.SemaphoreType.DMA
-    sems = [dma((5,))] + [dma((26,))] * 8 + [dma((44,))] * 4 + [dma((17,))] * 2
+    token = pltpu.SemaphoreType.REGULAR
+    sems = [vmem(400, 8, 128), token, token] + [dma] * 12
     return pl.pallas_call(
         kernel,
         out_shape=jax.ShapeDtypeStruct((BX, BY, BZ), F32),
-        in_specs=[pl.BlockSpec(memory_space=pl.ANY)],
-        out_specs=pl.BlockSpec(memory_space=pl.ANY),
+        in_specs=[pl.BlockSpec(memory_space=pltpu.HBM)],
+        out_specs=pl.BlockSpec(memory_space=pltpu.VMEM),
         scratch_shapes=level0 + level1 + level2 + packs + recv0 + recv1 + recv2 + gather + sems,
         compiler_params=pltpu.CompilerParams(
             collective_id=0, has_side_effects=True, vmem_limit_bytes=48 * 1024 * 1024

time: 54.7 us -> 48.6 us (0.89)
  Pallas kernels: 52.9 us -> 46.8 us
    pallas_call x1, Pallas kernels: 52.9 us -> 46.8 us  [on_device(): pl.pallas_call(kernel, out_shape=jax.ShapeDtypeStruct((BX, BY, BZ), F32),...]
where the time goes in v3:
time: 48.6 us; the launch traced here: 48.5 us
  Pallas kernels  46.8 us (96%)
  local copies, waits for them, and re-layouts  1.65 us (3%)
    pallas_call x1, Pallas kernels, on_device(): pl.pallas_call(kernel, out_shape=jax.ShapeDtypeStruct((BX, BY, BZ), F32),...  46.8 us
    unnamed x3, local copies, waits for them, and re-layouts  1.65 us

profile of v3, /device:TPU:1, one launch (start us, length us, event | category | flops | bytes accessed | tf_op | source)
XLA Modules:
  0.0 48.5 jit_solution(4101383009494231535)
XLA Ops:
  0.0 0.0 copy-start
  0.0 0.9 %copy-done = f32[32,16,128]{2,1,0:T(8,128)S(1)} copy-done((f32[32,16,128]{2,1,0:T(8,128)S(1)}, f32[32,16,128]{2,1,0:T(8,128)}, u32[]{:S(2)}) %copy-start) | copy-done | bytes 262168
  1.0 46.8 %shard_map.17 = f32[32,16,128]{2,1,0:T(8,128)S(1)} custom-call(f32[32,16,128]{2,1,0:T(8,128)S(1)} %copy-done), custom_call_target="tpu_custom_call" | custom-call | tf_op jit(solution)/shard_map/pallas_call | solution.py:690
  47.8 0.7 %copy.3 = f32[32,16,128]{2,1,0:T(8,128)} copy(f32[32,16,128]{2,1,0:T(8,128)S(1)} %shard_map.17) | data formatting | bytes 524288
Async XLA Ops:
  0.0 0.9 %copy-start = (f32[32,16,128]{2,1,0:T(8,128)S(1)}, f32[32,16,128]{2,1,0:T(8,128)}, u32[]{:S(2)}) copy-start(f32[32,16,128]{2,1,0:T(8,128)} %f_hbm.1) | copy-start | bytes 786436

commit v4 on v3

--- a/solution.py
+++ b/solution.py
@@ -463,13 +463,13 @@
     t3[...] = jnp.where(row == iy, a3, 0.0)
 
     egy, egz, egx = [], [], []
-    for k in range(1, NGY):
+    for k in (4, 3, 5, 2, 6, 1, 7):
         peer = (ix, lax.rem(iy + k, NGY), iz)
         egy.append(pltpu.make_async_remote_copy(t3, gy_r.at[k - 1], s_all, r_gy, peer, MESH))
-    for k in range(1, NGZ):
+    for k in (2, 1, 3):
         peer = (ix, iy, lax.rem(iz + k, NGZ))
         egz.append(pltpu.make_async_remote_copy(gzb.at[iz], gzb.at[iz], s_all, r_gz, peer, MESH))
-    for k in range(1, NGX):
+    for k in (4, 3, 5, 2, 6, 1, 7):
         peer = (lax.rem(ix + k, NGX), iy, iz)
         egx.append(pltpu.make_async_remote_copy(gzb, gxb.at[ix], s_all, r_gx, peer, MESH))
 
@@ -488,8 +488,6 @@
     for x in range(4):
         vx0[0, x] = vb0[4 + x, 8:24, :]
         vx0[1, x] = vb0[32 + x, 8:24, :]
-    arrive(r_f2b, units2b)
-    unpack2(ft2, f2_r, (-2, 2), clean(lev2), 2)
     wait_units(r_gy, 7)
     line = t3[...]
     for k in range(NGY - 1):
@@ -504,6 +502,8 @@
     start(ev1)
     start(ev0)
     gxb[ix] = gzb[...]
+    arrive(r_f2b, units2b)
+    unpack2(ft2, f2_r, (-2, 2), clean(lev2), 2)
     wait_units(r_gx, 28)
 
     for gx in range(NGX):
@@ -552,20 +552,27 @@
         par = (row // dy + zl // dz) & 1
         colours = (par == 0, par == 1)
 
-        def total(v, x):
-            c = v[x]
-            s = roll(c, dz, 1) * lo + roll(c, -dz, 1) * hi
-            s = s + (roll(c, dy, 0) * ylo + roll(c, -dy, 0) * yhi)
+        def beside(c, lo, hi, ylo, yhi):
+            z = roll(c, dz, 1) * lo + roll(c, -dz, 1) * hi
+            return z + (roll(c, dy, 0) * ylo + roll(c, -dy, 0) * yhi)
+
+        def fixed(v, x):
+            s = g[x]
             if x > 0:
                 s = s + v[x - 1]
             if x < n - 1:
                 s = s + v[x + 1]
             return s
 
+        weights = [[jnp.where(c, w * INV, 0.0) for w in (lo, hi, ylo, yhi)] for c in colours]
+
         def sweep(v, colour):
-            return [
-                jnp.where(colours[(x + colour) % 2], (g[x] + total(v, x)) * INV, v[x]) for x in range(n)
-            ]
+            out = []
+            for x in range(n):
+                c = (x + colour) % 2
+                base = jnp.where(colours[c], fixed(v, x) * INV, v[x])
+                out.append(base + beside(v[x], *weights[c]))
+            return out
 
         v = [jnp.where(colours[x % 2], g[x] * INV, 0.0) for x in range(n)]
         v = sweep(v, 1)
@@ -574,7 +581,7 @@
                 v = sweep(sweep(v, 0), 1)
             return v
         v = sweep(sweep(v, 0), 1)
-        r = [g[x] - (CENTRE * v[x] - total(v, x)) for x in range(n)]
+        r = [(fixed(v, x) - CENTRE * v[x]) + beside(v[x], lo, hi, ylo, yhi) for x in range(n)]
         coarse = []
         for x in range(n // 2):
             t = r[2 * x] + r[2 * x + 1]
@@ -696,7 +703,7 @@
         compiler_params=pltpu.CompilerParams(
             collective_id=0, has_side_effects=True, vmem_limit_bytes=48 * 1024 * 1024
         ),
-    )(density)
+    )(pltpu.with_memory_space_constraint(density, pltpu.HBM))
 
 
 def solution(mesh):

time: 48.6 us -> 46.8 us (0.963)
  local copies, waits for them, and re-layouts: 1.65 us -> 0.71 us
  Pallas kernels: 46.8 us -> 46 us
    unnamed x3 -> x1, local copies, waits for them, and re-layouts: 1.65 us -> 0.71 us
    pallas_call x1, Pallas kernels: 46.8 us -> 46 us  [on_device(): pl.pallas_call(kernel, out_shape=jax.ShapeDtypeStruct((BX, BY, BZ), F32),...]
where the time goes in v4:
time: 46.8 us; the launch traced here: 46.7 us
  Pallas kernels  46 us (98%)
  local copies, waits for them, and re-layouts  0.71 us (2%)
    pallas_call x1, Pallas kernels, on_device(): pl.pallas_call(kernel, out_shape=jax.ShapeDtypeStruct((BX, BY, BZ), F32),...  46 us

profile of v4, /device:TPU:1, one launch (start us, length us, event | category | flops | bytes accessed | tf_op | source)
XLA Modules:
  0.0 46.7 jit_solution(3574093857828417938)
XLA Ops:
  0.0 46.0 %shard_map.17 = f32[32,16,128]{2,1,0:T(8,128)S(1)} custom-call(f32[32,16,128]{2,1,0:T(8,128)} %f_hbm.1), custom_call_target="tpu_custom_call" | custom-call | tf_op jit(solution)/shard_map/pallas_call | solution.py:697
  46.0 0.7 %copy.3 = f32[32,16,128]{2,1,0:T(8,128)} copy(f32[32,16,128]{2,1,0:T(8,128)S(1)} %shard_map.17) | data formatting | bytes 524288

commit v5 on v4

--- a/solution.py
+++ b/solution.py
@@ -57,9 +57,9 @@
 
 def kernel(
     f_hbm, out,
-    f0, p0, fr0, fb0, vr0, vb0, k0, s0, pe0,
-    fr1, fb1, vr1, vb1, k1, s1, pe1, tmp1,
-    fr2, fb2, vr2, vb2, k2, s2, pe2, tmp2,
+    f0, p0, fr0, fb0, vr0, vb0, rest0, k0, s0, pe0,
+    fr1, fb1, vr1, vb1, rest1, k1, s1, pe1, tmp1,
+    fr2, fb2, vr2, vb2, rest2, k2, s2, pe2, tmp2,
     fy0, fz0, vy0, vz0, vx0, fk1, fz1, vk1, vz1, ft2, vt2,
     fx_r, fy_r, fxy_r, fz_r, vx_r, vy_r, vxy_r, vz_r,
     f1x_r, f1y_r, f1xy_r, f1z_r, v1x_r, v1y_r, v1xy_r, v1z_r,
@@ -106,8 +106,8 @@
     signed = jnp.where(l32 < 96, l32, l32 - 128)
 
     class Level:
-        def __init__(self, fr, fb, vr, vb, k, first, main, rows, window, odd, start, total):
-            self.fr, self.fb, self.vr, self.vb, self.k = fr, fb, vr, vb, k
+        def __init__(self, fr, fb, vr, vb, rest, k, first, main, rows, window, odd, start, total):
+            self.fr, self.fb, self.vr, self.vb, self.rest, self.k = fr, fb, vr, vb, rest, k
             self.first, self.main, self.rows, self.window = first, main, rows, window
             self.odd, self.start, self.total = odd, start, total
             self.planes = main + 2 * first
@@ -121,27 +121,40 @@
         def even(self, i, lo, hi):
             return (iota((hi - lo, 128), 0) + (lo + i + self.odd)) % 2 == 0
 
-    lev0 = Level(fr0, fb0, vr0, vb0, k0, 4, BX, (8, 24), (4, 28), 0, ix * BX - 4, NGX * BX)
-    lev1 = Level(fr1, fb1, vr1, vb1, k1, 6, 16, (16, 24), (8, 32), 0, ix * 16 - 6, NGX * 16)
-    lev2 = Level(fr2, fb2, vr2, vb2, k2, 7, 4, (16, 24), (8, 32), 1, iy * 4 - 7, NGY * 4)
+    lev0 = Level(fr0, fb0, vr0, vb0, rest0, k0, 4, BX, (8, 24), (4, 28), 0, ix * BX - 4, NGX * BX)
+    lev1 = Level(fr1, fb1, vr1, vb1, rest1, k1, 6, 16, (16, 24), (8, 32), 0, ix * 16 - 6, NGX * 16)
+    lev2 = Level(fr2, fb2, vr2, vb2, rest2, k2, 7, 4, (16, 24), (8, 32), 1, iy * 4 - 7, NGY * 4)
 
     def around(level, src, i, lo, hi, red):
-        c = src[i, lo:hi, :]
-        up, down = roll(c, 1, 1), roll(c, -1, 1)
+        c0, c1 = src[i, lo:hi, :], src[i + 1, lo:hi, :]
         even = level.even(i, lo, hi)
-        z = jnp.where(even, up, down) if red else jnp.where(even, down, up)
-        s = (src[i - 1, lo:hi, :] + src[i + 1, lo:hi, :]) + (
-            src[i, lo - 1 : hi - 1, :] + src[i, lo + 1 : hi + 1, :]
+        first, second = (c0, c1) if red else (c1, c0)
+        up = roll(jnp.where(even, first, second), 1, 1)
+        down = roll(jnp.where(even, second, first), -1, 1)
+        z0, z1 = jnp.where(even, up, down), jnp.where(even, down, up)
+        if not red:
+            z0, z1 = z1, z0
+
+        def plane(j, other, c, z):
+            s = (other + src[j, lo - 1 : hi - 1, :]) + src[j, lo + 1 : hi + 1, :]
+            return s + BETA1 * (c + z)
+
+        return (
+            plane(i, src[i - 1, lo:hi, :] + c1, c0, z0),
+            plane(i + 1, c0 + src[i + 2, lo:hi, :], c1, z1),
         )
-        return s + BETA1 * (c + z)
-
-    def half(level, lo, hi, red, rows=None):
+
+    def half(level, lo, hi, red, rows=None, keep=False):
         dst, src = (level.vr, level.vb) if red else (level.vb, level.vr)
         source = level.fr if red else level.fb
         a, b = rows or level.window
-        for i in range(lo, hi):
-            s = source[i, a:b, :] + around(level, src, i, a, b, red)
-            dst[i, a:b, :] = s * level.coefficient(i, a, b)
+        for i in range(lo, hi, 2):
+            for j, s in enumerate(around(level, src, i, a, b, red)):
+                s = source[i + j, a:b, :] + s
+                v = s * level.coefficient(i + j, a, b)
+                dst[i + j, a:b, :] = v
+                if keep and level.first <= i + j < level.first + level.main:
+                    level.rest[i + j, a:b, :] = s - CENTRE * v
 
     def first_half(level, lo, hi):
         a, b = level.window
@@ -153,14 +166,14 @@
         first_half(level, n - 4, m + 4)
         half(level, n - 3, m + 3, False)
         half(level, n - 2, m + 2, True)
-        half(level, n - 1, m + 1, False)
+        half(level, n - 1, m + 1, False, keep=True)
 
     def residual(level, i):
         a, b = level.rows
-        vr, vb = level.vr[i, a:b, :], level.vb[i, a:b, :]
-        red = level.fr[i, a:b, :] - (CENTRE * vr - around(level, level.vb, i, a, b, True))
-        black = level.fb[i, a:b, :] - (CENTRE * vb - around(level, level.vr, i, a, b, False))
-        return red + black
+        total = level.rest[i, a:b, :] + level.rest[i + 1, a:b, :]
+        for j, s in enumerate(around(level, level.vb, i, a, b, True)):
+            total = total + (level.fr[i + j, a:b, :] - (CENTRE * level.vr[i + j, a:b, :] - s))
+        return total
 
     def split_rows(a, even):
         return jnp.concatenate([jnp.where(even, a, 0.0), jnp.where(even, 0.0, a)], axis=1)
@@ -196,7 +209,7 @@
             yp[1, x // 2, half_tile, :] = p[12:16]
             t = roll(p, 2 * x, 1)
             lo = jnp.where(slot == x, t, lo)
-            hi = jnp.where(slot == (x - 1) % BX, roll(p, 64, 1) if x == 0 else t, hi)
+            hi = jnp.where(slot == (x - 1) % BX, t, hi)
         zp[0] = lo
         zp[1] = hi
 
@@ -259,7 +272,6 @@
                 low = zr[Z18.index((nx, ny, -1)), src : src + num, :]
                 high = zr[Z18.index((nx, ny, 1)), src : src + num, :]
                 lanes = iota((num, 128), 1)
-                mixed = [jnp.where(lanes < 64, high, low), jnp.where(lanes < 64, low, high)]
                 xs = range(28, 32) if nx < 0 else (range(32) if nx == 0 else range(4))
                 for x in xs:
                     if ny == 0:
@@ -271,16 +283,11 @@
                             p = xyr[XY4.index((nx, ny)), (x % 4) // 2]
                         if (x % 2 == 0) == (ny < 0):
                             p = roll(p, 4, 0)
-                    for colour in range(colours):
-                        if x == 0:
-                            a = roll(high, 64 if colour == 0 else 0, 1)
-                            b = roll(low, 0 if colour == 0 else 64, 1)
-                            e = jnp.where(lanes < 96, a, b)
-                        else:
-                            e = roll(mixed[colour], (64 if colour == 0 else 0) - 2 * x, 1)
-                        q = p if colour == 0 else roll(p, 64, 1)
-                        i = 32 * nx + x + 4
-                        put(colour, i, dst, num, jnp.where(lanes < 64, q, e))
+                    e = roll(jnp.where((lanes % 64) // 2 == x, high, low), 64 - 2 * x, 1)
+                    i = 32 * nx + x + 4
+                    put(0, i, dst, num, jnp.where(lanes < 64, p, e))
+                    if colours == 2:
+                        put(1, i, dst, num, roll(jnp.where(lanes < 64, e, p), 64, 1))
 
     def clean(level):
         def put(colour, i, dst, num, value):
@@ -327,13 +334,9 @@
     for ref in (vr0, vb0, vr1, vb1, vr2, vb2, pe0, pe1, pe2, v3, tmp2):
         zero(ref)
 
-    split1 = iota((256, 256), 1)
-    k1i = iota((256, 256), 0)
-    z1i = k1i % 128
-    red1 = (z1i + k1i // 128) % 2 == 0
-    packed = (split1 < 128) & (split1 % 64 == z1i // 2 + jnp.where(red1, 0, 32))
-    apart = (split1 >= 128) & (split1 - 128 == z1i // 2 + jnp.where(red1, 0, 64))
-    to_pairs1 = jnp.where((z1i < 64) & (packed | apart), 0.5, 0.0).astype(BF16)
+    to_pairs1 = jnp.where(
+        (z256 < 64) & (c128 % 32 == z256 // 2) & ((c128 < 64) == red256), 0.5, 0.0
+    ).astype(BF16)
     to_pairs2 = jnp.where(
         (z256 < 32) & (c128 % 32 == z256 // 2 + jnp.where(red256, 0, 16)), 0.5, 0.0
     ).astype(BF16)
@@ -346,7 +349,7 @@
     unpack0(lambda x: p0[x], fx_r, fy_r, fxy_r, fz_r, clean(lev0), 2)
     smooth_down(lev0)
     for x in range(16):
-        s0[x] = residual(lev0, 4 + 2 * x) + residual(lev0, 5 + 2 * x)
+        s0[x] = residual(lev0, 4 + 2 * x)
 
     rows = []
     for x in range(16):
@@ -359,9 +362,8 @@
         hi = jnp.zeros((8, 128), F32)
         for x in range(16):
             p = plane(x)
-            here = (lane % 64) // 3 == x
-            lo = jnp.where(here, roll(p, 3 * x, 1), lo)
-            hi = jnp.where(here, roll(p, 3 * x - 29, 1), hi)
+            lo = jnp.where((lane % 64) // 3 == x, roll(p, 3 * x, 1), lo)
+            hi = jnp.where(((lane + 35) % 64) // 3 == x, roll(p, 3 * x + 64, 1), hi)
         zp[0] = lo
         zp[1] = hi
 
@@ -389,17 +391,18 @@
                     tile = x // 2 - 5 if nx < 0 else x // 2
                     mid = xr[side(nx), tile] if ny == 0 else xyr[XY4.index((nx, ny)), tile]
                 low, high = zr[Z18.index((nx, ny, -1))], zr[Z18.index((nx, ny, 1))]
+                at_x = 32 * (x % 2)
+                e = roll(jnp.where((lane % 64) // 3 == x, high, low), at_x + 32 - 3 * x, 1)
                 for colour in range(colours):
-                    a = roll(mid, -64 * (x % 2) - 32 * colour, 1)
-                    b = roll(high, 32 - 3 * x - 64 * colour, 1)
-                    c = roll(low, 125 - 3 * x - 64 * colour, 1)
-                    put(colour, xe, 16 + 8 * ny, 8, jnp.where(lane < 32, a, jnp.where(lane < 64, b, c)))
+                    first = at_x + 64 * colour
+                    value = jnp.where((lane >= first) & (lane < first + 32), mid, e)
+                    put(colour, xe, 16 + 8 * ny, 8, roll(value, -first, 1))
 
     ef1 = copies1(fk1, fz1, f1x_r, f1y_r, f1xy_r, f1z_r, s_all, r_f1)
     ev1 = copies1(vk1, vz1, v1x_r, v1y_r, v1xy_r, v1z_r, s_all, r_v1)
     for t in range(8):
-        fk1[t] = jnp.where(lane < 64, b1[16 * t : 16 * t + 8, 0:128], b1[16 * t + 8 : 16 * t + 16, 0:128])
-    zpack1(lambda x: b1[8 * x : 8 * x + 8, 128:256], fz1)
+        fk1[t] = jnp.where(lane % 64 < 32, b1[16 * t : 16 * t + 8], b1[16 * t + 8 : 16 * t + 16])
+    zpack1(lambda x: b1[8 * x : 8 * x + 8], fz1)
     start(ef1)
     arrive(r_f1, units1)
     pl.semaphore_wait(tok, jnp.where((ix > 1) & (ix < NGX - 2), 2, 1) + far_y)
@@ -407,7 +410,7 @@
     unpack1(fk1, f1x_r, f1y_r, f1xy_r, f1z_r, clean(lev1), 2)
     smooth_down(lev1)
     for x in range(8):
-        s1[8 * x : 8 * x + 8, :] = residual(lev1, 6 + 2 * x) + residual(lev1, 7 + 2 * x)
+        s1[8 * x : 8 * x + 8, :] = residual(lev1, 6 + 2 * x)
 
     rows = []
     for y in range(4):
@@ -455,7 +458,7 @@
     smooth_down(lev2)
 
     for y in range(2):
-        s2[8 * y : 8 * y + 8, :] = residual(lev2, 7 + 2 * y) + residual(lev2, 8 + 2 * y)
+        s2[8 * y : 8 * y + 8, :] = residual(lev2, 7 + 2 * y)
     a3 = s2[pl.ds(0, 8, stride=2), :] + s2[pl.ds(1, 8, stride=2), :]
     a3 = jnp.where(lane < 16, 0.5 * a3, 0.0)
     a3 = pltpu.roll(a3, 0, 1, stride=16, stride_axis=0)
@@ -482,7 +485,7 @@
         acc = jnp.where(lane // 32 == y, roll(vb2[7 + y, 16:24, :], 32 * y, 1), acc)
     vt2[...] = acc
     for t in range(8):
-        vk1[t] = jnp.where(lane < 64, vb1[6 + 2 * t, 16:24, :], roll(vb1[7 + 2 * t, 16:24, :], 64, 1))
+        vk1[t] = jnp.where(lane % 64 < 32, vb1[6 + 2 * t, 16:24, :], roll(vb1[7 + 2 * t, 16:24, :], 32, 1))
     zpack1(lambda x: vb1[6 + x, 16:24, :], vz1)
     pack0(lambda x: vb0[4 + x, 8:24, :], vy0, vz0)
     for x in range(4):
@@ -682,9 +685,9 @@
         return pltpu.VMEM(shape, F32)
 
     coef = vmem(2, 32, 128)
-    level0 = [vmem(BX, BY, BZ)] * 2 + [vmem(40, 32, 128)] * 4 + [coef, vmem(16, 16, 128), vmem(20, 32, 128)]
-    level1 = [vmem(28, 40, 128)] * 4 + [coef, vmem(64, 128), vmem(14, 32, 128), vmem(288, 128)]
-    level2 = [vmem(18, 40, 128)] * 4 + [coef, vmem(16, 128), vmem(10, 32, 128), vmem(2, 128, 128)]
+    level0 = [vmem(BX, BY, BZ)] * 2 + [vmem(40, 32, 128)] * 5 + [coef, vmem(16, 16, 128), vmem(20, 32, 128)]
+    level1 = [vmem(28, 40, 128)] * 5 + [coef, vmem(64, 128), vmem(14, 32, 128), vmem(288, 128)]
+    level2 = [vmem(18, 40, 128)] * 5 + [coef, vmem(16, 128), vmem(10, 32, 128), vmem(2, 128, 128)]
     packs = [vmem(2, 16, 8, 128), vmem(2, 16, 128)] * 2 + [vmem(2, 4, 16, 128)] + [vmem(8, 8, 128), vmem(2, 8, 128)] * 2
     packs += [vmem(8, 128)] * 2
     recv0 = [vmem(2, 4, 16, 128), vmem(2, 16, 8, 128), vmem(4, 2, 8, 128), vmem(18, 16, 128)] * 2

time: 46.8 us -> 46.1 us (0.985)
  Pallas kernels: 46 us -> 45.3 us
    pallas_call x1, Pallas kernels: 46 us -> 45.3 us  [on_device(): pl.pallas_call(kernel, out_shape=jax.ShapeDtypeStruct((BX, BY, BZ), F32),...]
where the time goes in v5:
time: 46.1 us; the launch traced here: 46 us
  Pallas kernels  45.3 us (98%)
  local copies, waits for them, and re-layouts  0.71 us (2%)
    pallas_call x1, Pallas kernels, on_device(): pl.pallas_call(kernel, out_shape=jax.ShapeDtypeStruct((BX, BY, BZ), F32),...  45.3 us

profile of v5, /device:TPU:1, one launch (start us, length us, event | category | flops | bytes accessed | tf_op | source)
XLA Modules:
  0.0 46.0 jit_solution(3768068258483504085)
XLA Ops:
  0.0 45.3 %shard_map.17 = f32[32,16,128]{2,1,0:T(8,128)S(1)} custom-call(f32[32,16,128]{2,1,0:T(8,128)} %f_hbm.1), custom_call_target="tpu_custom_call" | custom-call | tf_op jit(solution)/shard_map/pallas_call | solution.py:700
  45.3 0.7 %copy.3 = f32[32,16,128]{2,1,0:T(8,128)} copy(f32[32,16,128]{2,1,0:T(8,128)S(1)} %shard_map.17) | data formatting | bytes 524288

commit v6 on v5

--- a/solution.py
+++ b/solution.py
@@ -57,7 +57,7 @@
 
 def kernel(
     f_hbm, out,
-    f0, p0, fr0, fb0, vr0, vb0, rest0, k0, s0, pe0,
+    f0, p0, turned, fr0, fb0, vr0, vb0, rest0, k0, s0, pe0,
     fr1, fb1, vr1, vb1, rest1, k1, s1, pe1, tmp1,
     fr2, fb2, vr2, vb2, rest2, k2, s2, pe2, tmp2,
     fy0, fz0, vy0, vz0, vx0, fk1, fz1, vk1, vz1, ft2, vt2,
@@ -276,18 +276,18 @@
                 for x in xs:
                     if ny == 0:
                         p = own(x) if nx == 0 else xr[side(nx), x % 4]
+                    elif nx == 0:
+                        p = yr[side(ny), x // 2]
                     else:
-                        if nx == 0:
-                            p = yr[side(ny), x // 2]
-                        else:
-                            p = xyr[XY4.index((nx, ny)), (x % 4) // 2]
-                        if (x % 2 == 0) == (ny < 0):
-                            p = roll(p, 4, 0)
-                    e = roll(jnp.where((lanes % 64) // 2 == x, high, low), 64 - 2 * x, 1)
+                        p = xyr[XY4.index((nx, ny)), (x % 4) // 2]
+                    if ny != 0 and (x % 2 == 0) == (ny < 0):
+                        p = roll(p, 4, 0)
+                    mixed = jnp.where((lanes % 64) // 2 == x, high, low)
                     i = 32 * nx + x + 4
-                    put(0, i, dst, num, jnp.where(lanes < 64, p, e))
+                    put(0, i, dst, num, jnp.where(lanes < 64, p, roll(mixed, 64 - 2 * x, 1)))
                     if colours == 2:
-                        put(1, i, dst, num, roll(jnp.where(lanes < 64, e, p), 64, 1))
+                        q = turned[x] if nx == 0 and ny == 0 else roll(p, 64, 1)
+                        put(1, i, dst, num, jnp.where(lanes < 64, q, roll(mixed, -2 * x, 1)))
 
     def clean(level):
         def put(colour, i, dst, num, value):
@@ -343,6 +343,9 @@
     csign = jnp.where(cc2 < 96, cc2, cc2 - 128)
     wanted = ((csign + 128) // 2 - 64 + 64 * (csign % 2)) % 128
     from_pairs = jnp.where(same & (kk2 == wanted) & (csign >= -4) & (csign < 68), 1.0, 0.0).astype(BF16)
+
+    for x in range(BX):
+        turned[x] = roll(p0[x], 64, 1)
 
     arrive(r_f0, units0)
     token(tok, 2)
@@ -391,12 +394,11 @@
                     tile = x // 2 - 5 if nx < 0 else x // 2
                     mid = xr[side(nx), tile] if ny == 0 else xyr[XY4.index((nx, ny)), tile]
                 low, high = zr[Z18.index((nx, ny, -1))], zr[Z18.index((nx, ny, 1))]
-                at_x = 32 * (x % 2)
-                e = roll(jnp.where((lane % 64) // 3 == x, high, low), at_x + 32 - 3 * x, 1)
+                mixed = jnp.where((lane % 64) // 3 == x, high, low)
                 for colour in range(colours):
-                    first = at_x + 64 * colour
-                    value = jnp.where((lane >= first) & (lane < first + 32), mid, e)
-                    put(colour, xe, 16 + 8 * ny, 8, roll(value, -first, 1))
+                    a = roll(mid, -32 * (x % 2) - 64 * colour, 1)
+                    b = roll(mixed, 32 - 3 * x - 64 * colour, 1)
+                    put(colour, xe, 16 + 8 * ny, 8, jnp.where(lane < 32, a, b))
 
     ef1 = copies1(fk1, fz1, f1x_r, f1y_r, f1xy_r, f1z_r, s_all, r_f1)
     ev1 = copies1(vk1, vz1, v1x_r, v1y_r, v1xy_r, v1z_r, s_all, r_v1)
@@ -685,7 +687,7 @@
         return pltpu.VMEM(shape, F32)
 
     coef = vmem(2, 32, 128)
-    level0 = [vmem(BX, BY, BZ)] * 2 + [vmem(40, 32, 128)] * 5 + [coef, vmem(16, 16, 128), vmem(20, 32, 128)]
+    level0 = [vmem(BX, BY, BZ)] * 3 + [vmem(40, 32, 128)] * 5 + [coef, vmem(16, 16, 128), vmem(20, 32, 128)]
     level1 = [vmem(28, 40, 128)] * 5 + [coef, vmem(64, 128), vmem(14, 32, 128), vmem(288, 128)]
     level2 = [vmem(18, 40, 128)] * 5 + [coef, vmem(16, 128), vmem(10, 32, 128), vmem(2, 128, 128)]
     packs = [vmem(2, 16, 8, 128), vmem(2, 16, 128)] * 2 + [vmem(2, 4, 16, 128)] + [vmem(8, 8, 128), vmem(2, 8, 128)] * 2

time: 46.1 us -> 45.7 us (level)
  no operation moved by 1% of the time
where the time goes in v6:
time: 45.7 us; the launch traced here: 45.6 us
  Pallas kernels  44.9 us (98%)
  local copies, waits for them, and re-layouts  0.71 us (2%)
    pallas_call x1, Pallas kernels, on_device(): pl.pallas_call(kernel, out_shape=jax.ShapeDtypeStruct((BX, BY, BZ), F32),...  44.9 us

profile of v6, /device:TPU:1, one launch (start us, length us, event | category | flops | bytes accessed | tf_op | source)
XLA Modules:
  0.0 45.6 jit_solution(723463925522618853)
XLA Ops:
  0.0 44.9 %shard_map.17 = f32[32,16,128]{2,1,0:T(8,128)S(1)} custom-call(f32[32,16,128]{2,1,0:T(8,128)} %f_hbm.1), custom_call_target="tpu_custom_call" | custom-call | tf_op jit(solution)/shard_map/pallas_call | solution.py:702
  44.9 0.7 %copy.3 = f32[32,16,128]{2,1,0:T(8,128)} copy(f32[32,16,128]{2,1,0:T(8,128)S(1)} %shard_map.17) | data formatting | bytes 524288

commit v7 on v6

--- a/solution.py
+++ b/solution.py
@@ -687,9 +687,9 @@
         return pltpu.VMEM(shape, F32)
 
     coef = vmem(2, 32, 128)
-    level0 = [vmem(BX, BY, BZ)] * 3 + [vmem(40, 32, 128)] * 5 + [coef, vmem(16, 16, 128), vmem(20, 32, 128)]
-    level1 = [vmem(28, 40, 128)] * 5 + [coef, vmem(64, 128), vmem(14, 32, 128), vmem(288, 128)]
-    level2 = [vmem(18, 40, 128)] * 5 + [coef, vmem(16, 128), vmem(10, 32, 128), vmem(2, 128, 128)]
+    level0 = [vmem(BX, BY, BZ)] * 3 + [vmem(40, 32, 128)] * 5 + [coef, vmem(16, 16, 128), vmem(20, 40, 128)]
+    level1 = [vmem(28, 40, 128)] * 5 + [coef, vmem(64, 128), vmem(14, 40, 128), vmem(400, 128)]
+    level2 = [vmem(18, 40, 128)] * 5 + [coef, vmem(16, 128), vmem(10, 40, 128), vmem(2, 160, 128)]
     packs = [vmem(2, 16, 8, 128), vmem(2, 16, 128)] * 2 + [vmem(2, 4, 16, 128)] + [vmem(8, 8, 128), vmem(2, 8, 128)] * 2
     packs += [vmem(8, 128)] * 2
     recv0 = [vmem(2, 4, 16, 128), vmem(2, 16, 8, 128), vmem(4, 2, 8, 128), vmem(18, 16, 128)] * 2

time: 45.7 us -> 45.7 us (level)
  no operation moved by 1% of the time
where the time goes in v7:
time: 45.7 us; the launch traced here: 45.6 us
  Pallas kernels  44.9 us (98%)
  local copies, waits for them, and re-layouts  0.71 us (2%)
    pallas_call x1, Pallas kernels, on_device(): pl.pallas_call(kernel, out_shape=jax.ShapeDtypeStruct((BX, BY, BZ), F32),...  44.9 us

profile of v7, /device:TPU:1, one launch (start us, length us, event | category | flops | bytes accessed | tf_op | source)
XLA Modules:
  0.0 45.6 jit_solution(15109096238666494896)
XLA Ops:
  0.0 44.9 %shard_map.17 = f32[32,16,128]{2,1,0:T(8,128)S(1)} custom-call(f32[32,16,128]{2,1,0:T(8,128)} %f_hbm.1), custom_call_target="tpu_custom_call" | custom-call | tf_op jit(solution)/shard_map/pallas_call | solution.py:702
  44.9 0.7 %copy.3 = f32[32,16,128]{2,1,0:T(8,128)} copy(f32[32,16,128]{2,1,0:T(8,128)S(1)} %shard_map.17) | data formatting | bytes 524288
